TPU v7x, 8 devices: a whole 2x2x1 slice. The times are simulated.
8 devices in a mesh: graph: 1 (over z), col: 2 (over y), row: 4 (over x, core).
Axes of the slice: x: 2, y: 2, z: 1, core: 2. Of those that a mesh axis runs over, the one named last changes fastest.
Arguments:
- flow_init: float32 [4096, 4096], P(('graph', 'row'), 'col')
- flow_graph: float32 [4096, 4096], P(('graph', 'row'), 'col')
Outputs:
- output: float32 [4096, 4096], P(('graph', 'row'), 'col')
All inputs are finite; a program needn't handle non-finite values.
Results may differ from a plain program's by a relative error of at most 0.001.
Values are sent between devices in bfloat16 or wider.
A program may use at most 1 GiB of HBM per device.

v0:
```python
import jax
import jax.numpy as jnp
from jax import lax
from jax.sharding import PartitionSpec as P

ITERATIONS = 3


def solution(mesh):
    num_cols = mesh.shape["col"]
    block_spec = P(("graph", "row"), "col")

    def device_step(init_blk, graph_blk):
        mat_order = init_blk.shape[1] * num_cols
        graph_panel = lax.all_gather(graph_blk.astype(jnp.bfloat16), "row", axis=0, tiled=True)
        flow_blk = init_blk
        for _ in range(ITERATIONS):
            row_panel = lax.all_gather(flow_blk.astype(jnp.bfloat16), "col", axis=1, tiled=True)
            expanded = jnp.dot(row_panel, graph_panel, preferred_element_type=jnp.float32)
            inflated = expanded * expanded
            col_sum = lax.psum(jnp.sum(inflated, axis=0), "row")
            flow_blk = inflated * (mat_order / col_sum)
        return flow_blk

    return jax.shard_map(device_step, mesh=mesh, in_specs=(block_spec, block_spec), out_specs=block_spec, check_vma=False)
```

profile of v0, /device:TPU:0, one launch (start us, length us, event | category | flops | bytes accessed | tf_op | source)
XLA Modules:
  0.0 548.4 jit_solution(16792844273219262703)
XLA Ops:
  6.5 0.0 all-gather.5.cloned.1.call-start
  6.5 6.1 %convert_element_type.12 = bf16[1024,2048]{1,0:T(8,128)(2,1)} convert(f32[1024,2048]{1,0:T(8,128)} %param.2) | non-fusion elementwise | flops 2097152 | bytes 12582912 | tf_op jit(solution)/shard_map/convert_element_type | solution.py:18
  12.6 0.0 all-gather.5.cloned.1.call-update
  12.6 0.0 all-gather.7.cloned.1.call-start
  12.7 6.0 %convert_element_type.13 = bf16[1024,2048]{1,0:T(8,128)(2,1)} convert(f32[1024,2048]{1,0:T(8,128)} %param.3) | non-fusion elementwise | flops 2097152 | bytes 12582912 | tf_op jit(solution)/shard_map/convert_element_type | solution.py:15
  18.7 0.0 all-gather.7.cloned.1.call-update
  18.7 0.0 all-gather.9.cloned.1.call-start
  18.8 99.1 %all-gather.5.cloned.1.call-done = bf16[1024,4096]{1,0:T(8,128)(2,1)} async-done(((bf16[1024,2048]{1,0:T(8,128)(2,1)}), bf16[1024,4096]{1,0:T(8,128)(2,1)}) %all-gather.5.cloned.1.call-update) | async-done | bytes 8388624 | tf_op jit(solution)/shard_map/all_gather | solution.py:18
  117.9 105.7 %all-gather.7.cloned.1.call-done = bf16[4096,2048]{1,0:T(8,128)(2,1)} async-done(((bf16[1024,2048]{1,0:T(8,128)(2,1)}), bf16[4096,2048]{1,0:T(8,128)(2,1)}) %all-gather.7.cloned.1.call-update) | async-done | bytes 16777232 | tf_op jit(solution)/shard_map/all_gather | solution.py:15
  223.6 24.0 %multiply_reduce_fusion.2 = (f32[2048]{0:T(1024)S(1)}, f32[1024,2048]{1,0:T(8,128)}) fusion(bf16[1024,4096]{1,0:T(8,128)(2,1)} %all-gather.5.cloned.1.call-done, bf16[4096,2048]{1,0:T(8,128)(2,1)} %all-gather.7.cloned.1.call-done), kind=kOutput, calls=%fused_computation.5 | convolution fusion | flops 17184061440 | bytes 33562624 | tf_op jit(solution)/shard_map/dot_general | solution.py:19
  247.7 6.0 %psum.21 = f32[2048]{0:T(1024)S(1)} all-reduce(f32[2048]{0:T(1024)S(1)} %get-tuple-element.5), channel_id=1, replica_groups=mesh['graph'=1,'col'=2,'row'=4] {'row'}, use_global_device_ids=true, to_apply=%region_1.0 | all-reduce | flops 2048 | bytes 16384 | tf_op jit(solution)/shard_map/psum | solution.py:21
  253.6 6.6 %multiply_convert_fusion.1 = bf16[1024,2048]{1,0:T(8,128)(2,1)} fusion(f32[1024,2048]{1,0:T(8,128)} %get-tuple-element.6, f32[2048]{0:T(1024)S(1)} %broadcast_divide_fusion.2), kind=kLoop, calls=%fused_computation.1 | loop fusion | flops 6291456 | bytes 12591104 | tf_op jit(solution)/shard_map/convert_element_type | solution.py:18
  260.2 0.0 all-gather.9.cloned.1.call-update
  260.2 0.0 all-gather.11.cloned.1.call-start
  260.3 103.5 %all-gather.9.cloned.1.call-done = bf16[1024,4096]{1,0:T(8,128)(2,1)} async-done(((bf16[1024,2048]{1,0:T(8,128)(2,1)}), bf16[1024,4096]{1,0:T(8,128)(2,1)}) %all-gather.9.cloned.1.call-update) | async-done | bytes 8388624 | tf_op jit(solution)/shard_map/all_gather | solution.py:18
  363.7 24.0 %multiply_reduce_fusion.1 = (f32[2048]{0:T(1024)S(1)}, f32[1024,2048]{1,0:T(8,128)}) fusion(bf16[1024,4096]{1,0:T(8,128)(2,1)} %all-gather.9.cloned.1.call-done, bf16[4096,2048]{1,0:T(8,128)(2,1)} %all-gather.7.cloned.1.call-done), kind=kOutput, calls=%fused_computation.4 | convolution fusion | flops 17184061440 | bytes 33562624 | tf_op jit(solution)/shard_map/dot_general | solution.py:19
  387.7 6.4 %psum.22 = f32[2048]{0:T(1024)S(1)} all-reduce(f32[2048]{0:T(1024)S(1)} %get-tuple-element.7), channel_id=1, replica_groups=mesh['graph'=1,'col'=2,'row'=4] {'row'}, use_global_device_ids=true, to_apply=%region_3.0 | all-reduce | flops 2048 | bytes 16384 | tf_op jit(solution)/shard_map/psum | solution.py:21
  394.2 6.6 %multiply_convert_fusion = bf16[1024,2048]{1,0:T(8,128)(2,1)} fusion(f32[1024,2048]{1,0:T(8,128)} %get-tuple-element.8, f32[2048]{0:T(1024)S(1)} %broadcast_divide_fusion.1), kind=kLoop, calls=%fused_computation | loop fusion | flops 6291456 | bytes 12591104 | tf_op jit(solution)/shard_map/convert_element_type | solution.py:18
  400.7 0.0 all-gather.11.cloned.1.call-update
  400.7 102.1 %all-gather.11.cloned.1.call-done = bf16[1024,4096]{1,0:T(8,128)(2,1)} async-done(((bf16[1024,2048]{1,0:T(8,128)(2,1)}), bf16[1024,4096]{1,0:T(8,128)(2,1)}) %all-gather.11.cloned.1.call-update) | async-done | bytes 8388624 | tf_op jit(solution)/shard_map/all_gather | solution.py:18
  502.8 24.0 %multiply_reduce_fusion = (f32[2048]{0:T(1024)S(1)}, f32[1024,2048]{1,0:T(8,128)}) fusion(bf16[1024,4096]{1,0:T(8,128)(2,1)} %all-gather.11.cloned.1.call-done, bf16[4096,2048]{1,0:T(8,128)(2,1)} %all-gather.7.cloned.1.call-done), kind=kOutput, calls=%fused_computation.3 | convolution fusion | flops 17184061440 | bytes 33562624 | tf_op jit(solution)/shard_map/dot_general | solution.py:19
  526.8 6.4 %psum.23 = f32[2048]{0:T(1024)S(1)} all-reduce(f32[2048]{0:T(1024)S(1)} %get-tuple-element.9), channel_id=1, replica_groups=mesh['graph'=1,'col'=2,'row'=4] {'row'}, use_global_device_ids=true, to_apply=%region_5.0 | all-reduce | flops 2048 | bytes 16384 | tf_op jit(solution)/shard_map/psum | solution.py:21
  533.3 8.6 %multiply_multiply_fusion = f32[1024,2048]{1,0:T(8,128)} fusion(f32[1024,2048]{1,0:T(8,128)} %get-tuple-element.10, f32[2048]{0:T(1024)S(1)} %broadcast_divide_fusion), kind=kLoop, calls=%fused_computation.2 | loop fusion | flops 4194304 | bytes 16785408 | tf_op jit(solution)/shard_map/mul | solution.py:22
  (3 shorter events, 0.0 us)
Async XLA Ops:
  6.5 111.3 %all-gather.5.cloned.1.call-start = ((), (), s32[]{:S(2)}) async-start(), calls=%async_computation | async-start | bytes 12582912 | tf_op jit(solution)/shard_map/all_gather | solution.py:18
  12.6 211.0 %all-gather.7.cloned.1.call-start = ((), (), s32[]{:S(2)}) async-start(), calls=%async_computation.1 | async-start | bytes 20971520 | tf_op jit(solution)/shard_map/all_gather | solution.py:15
  18.7 345.0 %all-gather.9.cloned.1.call-start = ((), (), s32[]{:S(2)}) async-start(), calls=%async_computation.2 | async-start | bytes 12582912 | tf_op jit(solution)/shard_map/all_gather | solution.py:18
  260.2 242.6 %all-gather.11.cloned.1.call-start = ((), (), s32[]{:S(2)}) async-start(), calls=%async_computation.3 | async-start | bytes 12582912 | tf_op jit(solution)/shard_map/all_gather | solution.py:18
Sparse Core Ops, SparseCore 0:
  12.7 105.0 all-gather.4
  119.4 104.1 all-gather.6
  260.3 103.3 all-gather.8
  400.9 101.8 all-gather.10
where the time goes:
time: 549 us; the launch traced here: 548 us
  waiting for transfers between devices  410 us (75%)
  matrix products  72.1 us (13%)
  other arithmetic  33.8 us (6%)
  blocking collectives  18.8 us (3%)
  between operations  13.2 us (2%)
    all_gather x3, waiting for transfers between devices, device_step(): lax.all_gather(flow_blk.astype(jnp.bfloat16), 'col', axis=1, tiled=True)  305 us
    all_gather x1, waiting for transfers between devices, device_step(): lax.all_gather(graph_blk.astype(jnp.bfloat16), 'row', axis=0, tiled=True)  106 us
    dot_general x3, matrix products, device_step(): jnp.dot(row_panel, graph_panel, preferred_element_type=jnp.float32)  72.1 us
    convert_element_type x3, other arithmetic, device_step(): flow_blk.astype(jnp.bfloat16)  19.2 us
    psum x3, blocking collectives, device_step(): col_sum = lax.psum(jnp.sum(inflated, axis=0), 'row')  18.8 us
  transfers between devices with their start and end apart: 4, of which 4 were waited for; matrix products, arithmetic and copies ran while one was open for 1% of the time, Pallas kernels for 0%

commit v1 on v0

v1 whole, which is shorter than its diff:
```python
import functools

import jax
import jax.numpy as jnp
from jax import lax
from jax.experimental import pallas as pl
from jax.experimental.pallas import tpu as pltpu
from jax.sharding import PartitionSpec as P

MESH = pl.DeviceIdType.MESH
WIDTH = 256
PIECES = 2
TILE_M = 512
F32, BF16 = jnp.float32, jnp.bfloat16


def dot(a, b):
    return jnp.dot(a, b, preferred_element_type=F32)


def kernel(n_all, flow_ref, graph_ref, out_ref, sum_ref, g_ref,
           a0, a1, c1, mbuf, gcol, gt, gsend, sums, s1, s2,
           stage_sem, keep_sem, col_sem, gt_sem, out_sem,
           xown_r, xfwd_r, ya_r, yg_r, core_r, sum_r, s1_r, s2_r,
           xown_s, xfwd_s, ya_s, yg_s, cown_s, cfwd_s, sum_s, s1_s, s2_s):
    rows, cols = flow_ref.shape
    nh = cols // WIDTH
    depth = 4 * rows
    half = depth // 2
    kg_rows = 2 * WIDTH
    prow = rows // PIECES

    y = lax.axis_index("col")
    r = lax.axis_index("row")
    z = lax.axis_index("graph")
    x = lax.div(r, 2)
    c = lax.rem(r, 2)
    xn = (z, y, (1 - x) * 2 + c)
    yn = (z, 1 - y, r)
    cn = (z, y, x * 2 + 1 - c)
    dn = (z, y, (1 - x) * 2 + 1 - c)
    lx = x + y - 2 * x * y
    own = pl.multiple_of((lx * 2 + c) * rows, rows)
    oth = pl.multiple_of(((1 - lx) * 2 + c) * rows, rows)

    def remote(src, dst, send, recv, dev):
        return pltpu.make_async_remote_copy(
            src_ref=src, dst_ref=dst, send_sem=send, recv_sem=recv, device_id=dev, device_id_type=MESH)

    def stage_copy(k):
        src = graph_ref if k < nh else flow_ref
        j = k % nh
        return pltpu.make_async_copy(src.at[:, pl.ds(j * WIDTH, WIDTH)], c1.at[k], stage_sem.at[k])

    for j in range(nh):
        stage_copy(j).start()
        stage_copy(nh + j).start()

    bar = pltpu.get_barrier_semaphore()
    for dev in (xn, yn, cn, dn):
        pl.semaphore_signal(bar, inc=1, device_id=dev, device_id_type=MESH)
    pl.semaphore_wait(bar, 4)

    def send_own(j):
        mine = pl.ds(own, rows)
        remote(gsend.at[j], g_ref.at[j, mine], xown_s, xown_r.at[j], xn).start()
        piece = pl.ds(j * WIDTH, WIDTH)
        remote(a0.at[:, piece], a0.at[:, pl.ds(cols + j * WIDTH, WIDTH)], ya_s, ya_r, yn).start()
        remote(gsend.at[j], g_ref.at[j, mine], cown_s, core_r.at[j], cn).start()
        pltpu.make_async_copy(gsend.at[j], g_ref.at[j, mine], keep_sem).start()

    for j in range(nh):
        stage_copy(j).wait()
        gsend[j] = c1[j].astype(BF16)
        stage_copy(nh + j).wait()
        a0[:, pl.ds(j * WIDTH, WIDTH)] = c1[nh + j].astype(BF16)
        if j >= 1:
            send_own(j - 1)
    send_own(nh - 1)
    for j in range(nh):
        for p in range(PIECES):
            src = gsend.at[j, pl.ds(p * prow, prow)]
            dst = g_ref.at[nh + j, pl.ds(oth + p * prow, prow)]
            remote(src, dst, yg_s, yg_r.at[j, p], yn).start()

    pltpu.make_async_copy(gsend, gsend, keep_sem).wait()

    def relay_y(j, p):
        piece = g_ref.at[nh + j, pl.ds(own + p * prow, prow)]
        remote(piece, piece, yg_s, yg_r.at[j, p], yn).wait_recv()
        remote(piece, piece, xfwd_s, xfwd_r.at[j, p], xn).start()
        remote(piece, piece, cfwd_s, core_r.at[nh + j], cn).start()

    def relay_x(j, p):
        piece = g_ref.at[nh + j, pl.ds(oth + p * prow, prow)]
        remote(piece, piece, xfwd_s, xfwd_r.at[j, p], xn).wait_recv()
        remote(piece, piece, cfwd_s, core_r.at[nh + j], cn).start()

    def wait_core(q):
        both = g_ref.at[q, pl.ds(0, half)]
        remote(both, both, cfwd_s, core_r.at[q], cn).wait_recv()

    def col_copy(q):
        slot = lax.rem(q, 2)
        return pltpu.make_async_copy(g_ref.at[q], gcol.at[slot], col_sem.at[slot])

    def tile_copy(kg, n):
        src = g_ref.at[n, pl.ds(pl.multiple_of(kg * kg_rows, kg_rows), kg_rows)]
        return pltpu.make_async_copy(src, gt.at[n], gt_sem.at[n])

    m_tiles = rows // TILE_M

    def over_m(body):
        def go(i, carry):
            body(pl.ds(pl.multiple_of(i * TILE_M, TILE_M), TILE_M))
            return carry
        lax.fori_loop(0, m_tiles, go, 0)

    def first_half(q):
        wait_core(q)
        col_copy(q).start()
        col_copy(q).wait()
        slot = lax.rem(q, 2)

        def body(m):
            c1[q, m, :] = dot(a0[m, :cols], gcol[slot, :half, :])
        over_m(body)

    def early(j, carry):
        piece = g_ref.at[j, pl.ds(oth, rows)]
        remote(piece, piece, xown_s, xown_r.at[j], xn).wait_recv()
        remote(piece, piece, cfwd_s, core_r.at[j], cn).start()

        @pl.when(j >= 1)
        def _():
            first_half(j - 1)
        return carry
    lax.fori_loop(0, nh, early, 0)
    first_half(nh - 1)

    other_a = a0.at[:, pl.ds(cols, cols)]
    remote(other_a, other_a, ya_s, ya_r, yn).wait_recv()

    def add_product(kg, n, g_tile):
        k = pl.ds(pl.multiple_of(kg * kg_rows, kg_rows), kg_rows)

        @pl.when(kg == 0)
        def _():
            c1[n] = dot(a1[:, k], g_tile[...])

        @pl.when(kg > 0)
        def _():
            c1[n] += dot(a1[:, k], g_tile[...])

    def col_tile(slot, kg):
        return gcol.at[slot, pl.ds(pl.multiple_of(kg * kg_rows, kg_rows), kg_rows)]

    def step(q, first, relay):
        slot = lax.rem(q, 2)
        kg = lax.div(q, 2)
        odd = lax.rem(q, 2) == 1

        @pl.when(odd)
        def _():
            lax.fori_loop(0, q, lambda n, t: (tile_copy(kg, n).start(), t)[1], 0)

        sums[q, r] = jnp.zeros((8, WIDTH), F32)

        def body(m):
            if first:
                v = c1[q, m, :] + dot(a0[m, cols:], gcol[slot, half:, :])
            else:
                v = dot(a0[m, :], gcol[slot])
            v = v * v
            mbuf[0, m, :] = v
            sums[q, r] += jnp.broadcast_to(jnp.sum(v, axis=0, keepdims=True), (8, WIDTH))
        over_m(body)

        for dev in (cn, xn, dn):
            remote(sums.at[q, r], sums.at[q, r], sum_s, sum_r.at[q], dev).start()

        def left(k, carry):
            add_product(k, q, col_tile(slot, k))
            return carry
        lax.fori_loop(0, kg, left, 0)

        relay()

        three = sums.at[q, pl.ds(0, 3)]
        remote(three, three, sum_s, sum_r.at[q], cn).wait_recv()
        total = (sums[q, 0] + sums[q, 1]) + (sums[q, 2] + sums[q, 3])
        scale = (n_all / total)[:1]
        a1[:, pl.ds(pl.multiple_of(q * WIDTH, WIDTH), WIDTH)] = (mbuf[0] * scale).astype(BF16)

        @pl.when(odd)
        def _():
            def right(n, carry):
                tile_copy(kg, n).wait()
                add_product(kg, n, gt.at[n])
                return carry
            lax.fori_loop(0, q, right, 0)
            add_product(kg, q, col_tile(slot, kg))

    col_copy(0).start()

    def own_step(q, carry):
        col_copy(q).wait()

        @pl.when(q + 1 < nh)
        def _():
            col_copy(q + 1).start()

        def relay():
            @pl.when(q == 2)
            def _():
                relay_y(0, 0)

            @pl.when(q == 4)
            def _():
                relay_y(0, 1)

            @pl.when(q == 6)
            def _():
                relay_y(1, 0)
                relay_x(0, 0)
        step(q, True, relay)
        return carry
    lax.fori_loop(0, nh, own_step, 0)

    def other_step(j, carry):
        q = nh + j

        @pl.when(j + 1 < nh)
        def _():
            relay_y(j + 1, 1)
        relay_x(j, 1)
        wait_core(q)
        col_copy(q).start()
        col_copy(q).wait()

        def relay():
            @pl.when(j + 2 < nh)
            def _():
                relay_y(j + 2, 0)

            @pl.when(j + 1 < nh)
            def _():
                relay_x(j + 1, 0)
        step(q, False, relay)
        return carry
    lax.fori_loop(0, nh, other_step, 0)

    col_copy(0).start()

    def square(n, carry):
        v = c1[n]
        v = v * v
        c1[n] = v
        s1[r, pl.ds(n, 1), :] = jnp.sum(v, axis=0, keepdims=True)
        return carry
    lax.fori_loop(0, 2 * nh, square, 0)
    for dev in (cn, xn, dn):
        remote(s1.at[r], s1.at[r], s1_s, s1_r, dev).start()
    remote(a0.at[:, pl.ds(0, cols)], a0.at[:, pl.ds(0, cols)], ya_s, ya_r, yn).wait_send()
    three = s1.at[pl.ds(0, 3)]
    remote(three, three, s1_s, s1_r, cn).wait_recv()

    def rescale(n, carry):
        line = pl.ds(n, 1)
        total = (s1[0, line, :] + s1[1, line, :]) + (s1[2, line, :] + s1[3, line, :])
        a0[:, pl.ds(pl.multiple_of(n * WIDTH, WIDTH), WIDTH)] = (c1[n] * (n_all / total)).astype(BF16)
        return carry
    lax.fori_loop(0, 2 * nh, rescale, 0)

    def out_copy(n):
        slot = lax.rem(n, 2)
        dst = out_ref.at[:, pl.ds(pl.multiple_of(n * WIDTH, WIDTH), WIDTH)]
        return pltpu.make_async_copy(mbuf.at[slot], dst, out_sem.at[slot])

    def last(n, carry):
        slot = lax.rem(n, 2)
        col_copy(n).wait()

        @pl.when(n + 1 < nh)
        def _():
            col_copy(n + 1).start()

        @pl.when(n >= 2)
        def _():
            out_copy(n - 2).wait()
        s2[r, pl.ds(n, 1), :] = jnp.zeros((1, WIDTH), F32)

        def body(m):
            v = dot(a0[m, :], gcol[slot])
            v = v * v
            mbuf[slot, m, :] = v
            s2[r, pl.ds(n, 1), :] += jnp.sum(v, axis=0, keepdims=True)
        over_m(body)
        out_copy(n).start()
        return carry
    lax.fori_loop(0, nh, last, 0)

    for dev in (cn, xn, dn):
        remote(s2.at[r], s2.at[r], s2_s, s2_r, dev).start()
    out_copy(nh - 2).wait()
    out_copy(nh - 1).wait()
    three = s2.at[pl.ds(0, 3)]
    remote(three, three, s2_s, s2_r, cn).wait_recv()
    sum_ref[...] = (s2[0] + s2[1]) + (s2[2] + s2[3])

    remote(gsend, gsend, xown_s, xown_r.at[0], xn).wait_send()
    remote(gsend, gsend, yg_s, xown_r.at[0], yn).wait_send()
    remote(gsend, gsend, cown_s, xown_r.at[0], cn).wait_send()
    fwd = g_ref.at[pl.ds(0, nh), pl.ds(0, rows)]
    remote(fwd, fwd, xfwd_s, xown_r.at[0], xn).wait_send()
    fwd = g_ref.at[pl.ds(0, nh), pl.ds(0, 3 * rows)]
    remote(fwd, fwd, cfwd_s, xown_r.at[0], cn).wait_send()
    part = sums.at[:, pl.ds(0, 3)]
    remote(part, part, sum_s, xown_r.at[0], cn).wait_send()
    remote(s1.at[pl.ds(0, 3)], s1.at[pl.ds(0, 3)], s1_s, xown_r.at[0], cn).wait_send()
    remote(s2.at[pl.ds(0, 3)], s2.at[pl.ds(0, 3)], s2_s, xown_r.at[0], cn).wait_send()


def solution(mesh):
    block_spec = P(("graph", "row"), "col")

    def device_step(init_blk, graph_blk):
        rows, cols = init_blk.shape
        n_all = 2 * cols
        nh = cols // WIDTH
        dma = pltpu.SemaphoreType.DMA
        any_spec = pl.BlockSpec(memory_space=pl.ANY)
        raw, col_sum, _ = pl.pallas_call(
            functools.partial(kernel, float(n_all)),
            out_shape=(
                jax.ShapeDtypeStruct((rows, cols), F32),
                jax.ShapeDtypeStruct((nh, WIDTH), F32),
                jax.ShapeDtypeStruct((2 * nh, n_all, WIDTH), BF16),
            ),
            in_specs=[any_spec, any_spec],
            out_specs=(any_spec, pl.BlockSpec(memory_space=pltpu.VMEM), any_spec),
            scratch_shapes=[
                pltpu.VMEM((rows, n_all), BF16),
                pltpu.VMEM((rows, n_all), BF16),
                pltpu.VMEM((2 * nh, rows, WIDTH), F32),
                pltpu.VMEM((2, rows, WIDTH), F32),
                pltpu.VMEM((2, n_all, WIDTH), BF16),
                pltpu.VMEM((2 * nh, 2 * WIDTH, WIDTH), BF16),
                pltpu.VMEM((nh, rows, WIDTH), BF16),
                pltpu.VMEM((2 * nh, 4, 8, WIDTH), F32),
                pltpu.VMEM((4, 2 * nh, WIDTH), F32),
                pltpu.VMEM((4, nh, WIDTH), F32),
                dma((2 * nh,)), dma, dma((2,)), dma((2 * nh,)), dma((2,)),
                dma((nh,)), dma((nh, PIECES)), dma, dma((nh, PIECES)), dma((2 * nh,)), dma((2 * nh,)), dma, dma,
                dma, dma, dma, dma, dma, dma, dma, dma, dma,
            ],
            compiler_params=pltpu.CompilerParams(
                collective_id=0, has_side_effects=True, vmem_limit_bytes=62 * 2**20),
            name="mcl",
        )(init_blk, graph_blk)
        return raw * (n_all / col_sum.reshape(cols))

    return jax.shard_map(device_step, mesh=mesh, in_specs=(block_spec, block_spec), out_specs=block_spec, check_vma=False)
```

time: 549 us -> 301 us (0.55)
  waiting for transfers between devices: 410 us -> 0 us
  Pallas kernels: 0 us -> 291 us
  matrix products: 72.1 us -> 0 us
  other arithmetic: 33.8 us -> 9.18 us
  blocking collectives: 18.8 us -> 0 us
  between operations: 13.2 us -> 0.01 us
    all_gather x4 -> x0, waiting for transfers between devices: 410 us -> none  [the longest x3 305 us: device_step(): lax.all_gather(flow_blk.astype(jnp.bfloat16), 'col', axis=1, tiled=True)]
    pallas_call x0 -> x1, Pallas kernels: none -> 291 us  [device_step(): pl.pallas_call(functools.partial(kernel, float(n_all)), out_shape=(jax.Sh...]
    dot_general x3 -> x0, matrix products: 72.1 us -> none  [device_step(): jnp.dot(row_panel, graph_panel, preferred_element_type=jnp.float32)]
    convert_element_type x4 -> x0, other arithmetic: 25.2 us -> none  [the longest x3 19.2 us: device_step(): flow_blk.astype(jnp.bfloat16)]
    psum x3 -> x0, blocking collectives: 18.8 us -> none  [device_step(): col_sum = lax.psum(jnp.sum(inflated, axis=0), 'row')]
  transfers between devices with their start and end apart: 4 -> 0, of which waited for: 4 -> 0; matrix products, arithmetic and copies ran while one was open for 1% -> 0% of each run, Pallas kernels for 0% -> 0%
where the time goes in v1:
time: 301 us
  Pallas kernels  291 us (97%)
  other arithmetic  9.18 us (3%)
    pallas_call x1, Pallas kernels, device_step(): pl.pallas_call(functools.partial(kernel, float(n_all)), out_shape=(jax.Sh...  291 us
    mul x1, other arithmetic, device_step(): return raw * (n_all / col_sum.reshape(cols))  8.47 us

profile of v1, /device:TPU:0, one launch (start us, length us, event | category | flops | bytes accessed | tf_op | source)
XLA Modules:
  0.0 300.5 jit_solution(2304738466908557203)
XLA Ops:
  0.0 291.3 %mcl.1 = (f32[1024,2048]{1,0:T(8,128)}, f32[8,256]{1,0:T(8,128)}, bf16[16,4096,256]{2,1,0:T(8,128)(2,1)}) custom-call(f32[1024,2048]{1,0:T(8,128)} %flow_ref.1, f32[1024,2048]{1,0:T(8,128)} %graph_ref.1), custom_call_target="tpu_custom_call" | custom-call | tf_op jit(solution)/shard_map/mcl/pallas_call | solution.py:333
  291.3 0.7 divide_bitcast_fusion
  292.1 8.5 %broadcast_multiply_fusion = f32[1024,2048]{1,0:T(8,128)} fusion(f32[1024,2048]{1,0:T(8,128)} %get-tuple-element.7, f32[2048]{0:T(1024)S(1)} %bitcast.3), kind=kLoop, calls=%fused_computation | loop fusion | flops 2097152 | bytes 16785408 | tf_op jit(solution)/shard_map/mul | solution.py:361
  (1 shorter events, 0.0 us)

commit v2 on v0

v2 whole, which is shorter than its diff:
```python
import contextlib
import functools

import jax
import jax.numpy as jnp
from jax import lax
from jax.experimental import pallas as pl
from jax.experimental.pallas import tpu as pltpu
from jax.sharding import PartitionSpec as P

MESH = pl.DeviceIdType.MESH
WIDTH = 256
PIECES = 4
F32, BF16 = jnp.float32, jnp.bfloat16


def nothing(name):
    return contextlib.nullcontext()


scope = nothing


def dot(a, b):
    return jnp.dot(a, b, preferred_element_type=F32)


def kernel(n_all, flow_ref, graph_ref, out_ref, sum_ref, g_ref,
           a0, a1, c1, mbuf, gown, gcol, gt, sums, s1, s2,
           stage_sem, col_sem, gt_sem, out_sem,
           xown_r, xfwd_r, ya_r, yg_r, core_r, sum_r, s1_r, s2_r,
           xown_s, xfwd_s, ya_s, yg_s, cown_s, cfwd_s, sum_s, s1_s, s2_s):
    rows, cols = flow_ref.shape
    nh = cols // WIDTH
    depth = 4 * rows
    half = depth // 2
    quad = half // 2
    kg_rows = 2 * WIDTH
    prow = rows // PIECES

    y = lax.axis_index("col")
    r = lax.axis_index("row")
    z = lax.axis_index("graph")
    x = lax.div(r, 2)
    c = lax.rem(r, 2)
    xn = (z, y, (1 - x) * 2 + c)
    yn = (z, 1 - y, r)
    cn = (z, y, x * 2 + 1 - c)
    dn = (z, y, (1 - x) * 2 + 1 - c)
    lx = x + y - 2 * x * y
    own = pl.multiple_of((lx * 2 + c) * rows, rows)
    oth = pl.multiple_of(((1 - lx) * 2 + c) * rows, rows)
    mine, theirs = pl.ds(own, rows), pl.ds(oth, rows)

    def remote(src, dst, send, recv, dev):
        return pltpu.make_async_remote_copy(
            src_ref=src, dst_ref=dst, send_sem=send, recv_sem=recv, device_id=dev, device_id_type=MESH)

    def chunk(q):
        return pl.ds(pl.multiple_of(q * WIDTH, WIDTH), WIDTH)

    def stage_copy(k):
        src = graph_ref if k < nh else flow_ref
        return pltpu.make_async_copy(src.at[:, pl.ds((k % nh) * WIDTH, WIDTH)], c1.at[k], stage_sem.at[k])

    def stage(j):
        if j < nh:
            stage_copy(j).start()
            stage_copy(nh + j).start()

    stage(0)
    bar = pltpu.get_barrier_semaphore()
    for dev in (xn, yn, cn, dn):
        pl.semaphore_signal(bar, inc=1, device_id=dev, device_id_type=MESH)
    stage(1)
    stage(2)

    def send_own(j):
        block = gown.at[j, mine]
        remote(block, block, xown_s, xown_r.at[j], xn).start()
        piece = pl.ds(j * WIDTH, WIDTH)
        remote(a0.at[:, piece], a0.at[:, pl.ds(cols + j * WIDTH, WIDTH)], ya_s, ya_r.at[j * 2 // nh], yn).start()
        remote(block, block, cown_s, core_r.at[j], cn).start()

    for j in range(nh):
        with scope("cast"):
            stage_copy(j).wait()
            gown[j, mine, :] = c1[j].astype(BF16)
            stage_copy(nh + j).wait()
            a0[:, pl.ds(j * WIDTH, WIDTH)] = c1[nh + j].astype(BF16)
            stage(j + 3)
            if j == 1:
                pl.semaphore_wait(bar, 4)
            if j >= 1:
                send_own(j - 1)
    send_own(nh - 1)
    for j in range(nh):
        for p in range(PIECES):
            src = gown.at[j, pl.ds(own + p * prow, prow)]
            dst = g_ref.at[j, pl.ds(oth + p * prow, prow)]
            remote(src, dst, yg_s, yg_r.at[j, p], yn).start()

    n_pieces = nh * PIECES

    def relay(k, offset, sem, recv, dev, forward):
        @pl.when((k >= 0) & (k < n_pieces))
        def _():
            j, p = lax.div(k, PIECES), lax.rem(k, PIECES)
            piece = g_ref.at[j, pl.ds(pl.multiple_of(offset + p * prow, prow), prow)]
            remote(piece, piece, sem, recv.at[j, p], dev).wait_recv()
            if forward:
                remote(piece, piece, xfwd_s, xfwd_r.at[j, p], xn).start()
            remote(piece, piece, cfwd_s, core_r.at[nh + j], cn).start()

    def relay_y(*ks):
        for k in ks:
            with scope("relay_y"):
                relay(jnp.int32(k), own, yg_s, yg_r, yn, True)

    def relay_x(*ks):
        for k in ks:
            with scope("relay_x"):
                relay(jnp.int32(k), oth, xfwd_s, xfwd_r, xn, False)

    def wait_core(q):
        with scope("wait_core"):
            both = gown.at[0, pl.ds(0, half)]
            remote(both, both, cfwd_s, core_r.at[q], cn).wait_recv()

    def col_copy(q):
        slot = lax.rem(q, 2)
        return pltpu.make_async_copy(g_ref.at[q - nh], gcol.at[slot], col_sem.at[slot])

    def k_rows(kg):
        return pl.ds(pl.multiple_of(kg * kg_rows, kg_rows), kg_rows)

    def tile_copy(kg, j):
        return pltpu.make_async_copy(g_ref.at[j, k_rows(kg)], gt.at[j], gt_sem.at[j])

    def loop(lo, hi, body):
        def go(i, carry):
            body(i)
            return carry
        lax.fori_loop(lo, hi, go, 0)

    def unrolled(n, width, body):
        def some(i):
            for t in range(width):
                body(i * width + t)
        loop(0, n, some)

    def first_half(q):
        wait_core(q)

        c1[q] = dot(a0[:, :cols], gown[q, :half, :])

    def third_quarter(q):
        c1[q] += dot(a0[:, cols:cols + quad], gown[q, half:half + quad, :])

    def wait_a(i):
        with scope("wait_a"):
            part = a0.at[:, pl.ds(0, quad)]
            remote(part, part, ya_s, ya_r.at[i], yn).wait_recv()

    def early(j):
        with scope("wait_xown"):
            block = gown.at[j, theirs]
            remote(block, block, xown_s, xown_r.at[j], xn).wait_recv()
        remote(block, block, cfwd_s, core_r.at[j], cn).start()

        @pl.when(j >= 1)
        def _():
            with scope("first_half"):
                first_half(j - 1)

        @pl.when(j == nh - 3)
        def _():
            wait_a(0)

        @pl.when(j >= nh - 3)
        def _():
            with scope("third_quarter"):
                first = 2 * (j - (nh - 3))
                third_quarter(first)
                third_quarter(first + 1)
    loop(0, nh, early)
    with scope("early_end"):
        third_quarter(nh - 2)
        first_half(nh - 1)
        third_quarter(nh - 1)
    wait_a(1)

    def add_product(kg, n, g_tile):
        @pl.when(kg == 0)
        def _():
            c1[n] = dot(a1[:, k_rows(kg)], g_tile[...])

        @pl.when(kg > 0)
        def _():
            c1[n] += dot(a1[:, k_rows(kg)], g_tile[...])

    def finish(q):
        with scope("finish"):
            three = sums.at[q, pl.ds(0, 3)]
            remote(three, three, sum_s, sum_r.at[q], cn).wait_recv()
            total = (sums[q, 0] + sums[q, 1]) + (sums[q, 2] + sums[q, 3])
            scale = (n_all / total)[:1]
            a1[:, chunk(q)] = (mbuf[lax.rem(q, 2)] * scale).astype(BF16)

    def step(q, first, after_first, after_left):
        slot = lax.rem(q, 2)
        done = lax.div(q, 2)
        even = slot == 0

        if not first:
            @pl.when(even)
            def _():
                loop(0, q - nh, lambda j: tile_copy(done - 1, j).start())

        with scope("c0"):
            if first:
                v = c1[q] + dot(a0[:, cols + quad:], gown[q, half + quad:, :])
            else:
                v = dot(a0[...], gcol[slot])
            v = v * v
            mbuf[slot] = v
            sums[q, r] = jnp.broadcast_to(jnp.sum(v, axis=0, keepdims=True), (8, WIDTH))
        for dev in (cn, xn, dn):
            remote(sums.at[q, r], sums.at[q, r], sum_s, sum_r.at[q], dev).start()

        after_first()

        @pl.when(q >= 1)
        def _():
            finish(q - 1)

        with scope("left"):
            if first:
                loop(0, done, lambda k: add_product(k, q, gown.at[q, k_rows(k)]))
            else:
                c1[q] = dot(a1[:, :cols], gcol[slot, :half, :])
                loop(nh // 2, done, lambda k: add_product(k, q, gcol.at[slot, k_rows(k)]))

        after_left()

        @pl.when(even & (q >= 2))
        def _():
            with scope("right"):
                kg = done - 1
                if first:
                    def pair(i):
                        for n in (2 * i, 2 * i + 1):
                            c1[n] += dot(a1[:, k_rows(kg)], gown[n, k_rows(kg), :])

                    @pl.when(kg == 0)
                    def _():
                        for n in (0, 1):
                            c1[n] = dot(a1[:, k_rows(0)], gown[n, k_rows(0), :])

                    @pl.when(kg > 0)
                    def _():
                        loop(0, done, pair)
                else:
                    def some(i):
                        for n in range(4):
                            c1[4 * i + n] += dot(a1[:, k_rows(kg)], gown[4 * i + n, k_rows(kg), :])
                    loop(0, nh // 4, some)

                    def pair(i):
                        for j in (2 * i, 2 * i + 1):
                            tile_copy(kg, j).wait()
                        for j in (2 * i, 2 * i + 1):
                            c1[nh + j] += dot(a1[:, k_rows(kg)], gt[j])
                    loop(0, done - nh // 2, pair)

    def own_step(q):
        def after_first():
            for at, ys, xs in ((1, (0,), ()), (2, (1,), ()), (4, (2,), ()), (5, (3,), (0, 1)), (6, (4,), ()), (7, (5,), (2,))):
                @pl.when(q == at)
                def _():
                    relay_y(*ys)
                    relay_x(*xs)
        step(q, True, after_first, lambda: None)
    loop(0, nh, own_step)
    relay_y(6)
    relay_x(3)
    wait_core(nh)
    col_copy(nh).start()

    def other_step(j):
        q = nh + j
        k = PIECES * j
        with scope("load"):
            col_copy(q).wait()

        def after_first():
            relay_y(k + 7)
            relay_x(k + 4, k + 5)

        def after_left():
            relay_y(k + 8)
            relay_x(k + 6)
        step(q, False, after_first, after_left)
        relay_y(k + 9)
        relay_x(k + 7)

        @pl.when(j + 1 < nh)
        def _():
            wait_core(q + 1)
            col_copy(q + 1).start()
        relay_y(k + 10)
    loop(0, nh, other_step)

    last_kg = nh - 1
    loop(0, nh, lambda j: tile_copy(last_kg, j).start())
    finish(2 * nh - 1)

    def close(n, g_tile):
        v = c1[n] + dot(a1[:, k_rows(last_kg)], g_tile[...])
        v = v * v
        c1[n] = v
        s1[r, pl.ds(n, 1), :] = jnp.sum(v, axis=0, keepdims=True)

    def close_other(j):
        tile_copy(last_kg, j).wait()
        close(nh + j, gt.at[j])
    with scope("close"):
        unrolled(nh // 4, 4, lambda n: close(n, gown.at[n, k_rows(last_kg)]))
        unrolled(nh // 4, 4, close_other)
    for dev in (cn, xn, dn):
        remote(s1.at[r], s1.at[r], s1_s, s1_r, dev).start()
    with scope("wait_s1"):
        remote(a0.at[:, pl.ds(0, cols)], a0.at[:, pl.ds(0, cols)], ya_s, ya_r.at[0], yn).wait_send()
        three = s1.at[pl.ds(0, 3)]
        remote(three, three, s1_s, s1_r, cn).wait_recv()

    def rescale(n):
        line = pl.ds(n, 1)
        total = (s1[0, line, :] + s1[1, line, :]) + (s1[2, line, :] + s1[3, line, :])
        a0[:, chunk(n)] = (c1[n] * (n_all / total)).astype(BF16)
    with scope("rescale"):
        loop(0, 2 * nh, rescale)

    def out_copy(n):
        slot = lax.rem(n, 2)
        return pltpu.make_async_copy(mbuf.at[slot], out_ref.at[:, chunk(n)], out_sem.at[slot])

    def last(n):
        slot = lax.rem(n, 2)

        @pl.when(n >= 2)
        def _():
            out_copy(n - 2).wait()
        v = dot(a0[...], gown[n])
        v = v * v
        mbuf[slot] = v
        s2[r, pl.ds(n, 1), :] = jnp.sum(v, axis=0, keepdims=True)
        out_copy(n).start()
    with scope("last"):
        loop(0, nh, last)

    for dev in (cn, xn, dn):
        remote(s2.at[r], s2.at[r], s2_s, s2_r, dev).start()

    def sent(ref, sem):
        remote(ref, ref, sem, s2_r, cn).wait_send()
    sent(gown.at[:, pl.ds(0, rows)], xown_s)
    sent(gown.at[:, pl.ds(0, rows)], yg_s)
    sent(gown.at[:, pl.ds(0, rows)], cown_s)
    sent(gown.at[:, pl.ds(0, rows)], xfwd_s)
    sent(gown.at[:, pl.ds(0, 3 * rows)], cfwd_s)
    sent(sums.at[:, pl.ds(0, 3)], sum_s)
    sent(s1.at[pl.ds(0, 3)], s1_s)
    out_copy(nh - 2).wait()
    out_copy(nh - 1).wait()
    with scope("wait_s2"):
        three = s2.at[pl.ds(0, 3)]
        remote(three, three, s2_s, s2_r, cn).wait()
    sum_ref[...] = (s2[0] + s2[1]) + (s2[2] + s2[3])


def solution(mesh):
    block_spec = P(("graph", "row"), "col")

    def device_step(init_blk, graph_blk):
        rows, cols = init_blk.shape
        n_all = 2 * cols
        nh = cols // WIDTH
        dma = pltpu.SemaphoreType.DMA
        any_spec = pl.BlockSpec(memory_space=pl.ANY)
        raw, col_sum, _ = pl.pallas_call(
            functools.partial(kernel, float(n_all)),
            out_shape=(
                jax.ShapeDtypeStruct((rows, cols), F32),
                jax.ShapeDtypeStruct((nh, WIDTH), F32),
                jax.ShapeDtypeStruct((nh, n_all, WIDTH), BF16),
            ),
            in_specs=[any_spec, any_spec],
            out_specs=(any_spec, pl.BlockSpec(memory_space=pltpu.VMEM), any_spec),
            scratch_shapes=[
                pltpu.VMEM((rows, n_all), BF16),
                pltpu.VMEM((rows, n_all), BF16),
                pltpu.VMEM((2 * nh, rows, WIDTH), F32),
                pltpu.VMEM((2, rows, WIDTH), F32),
                pltpu.VMEM((nh, n_all, WIDTH), BF16),
                pltpu.VMEM((2, n_all, WIDTH), BF16),
                pltpu.VMEM((nh, 2 * WIDTH, WIDTH), BF16),
                pltpu.VMEM((2 * nh, 4, 8, WIDTH), F32),
                pltpu.VMEM((4, 2 * nh, WIDTH), F32),
                pltpu.VMEM((4, nh, WIDTH), F32),
                dma((2 * nh,)), dma((2,)), dma((nh,)), dma((2,)),
                dma((nh,)), dma((nh, PIECES)), dma((2,)), dma((nh, PIECES)), dma((2 * nh,)), dma((2 * nh,)), dma, dma,
                dma, dma, dma, dma, dma, dma, dma, dma, dma,
            ],
            compiler_params=pltpu.CompilerParams(
                collective_id=0, has_side_effects=True, vmem_limit_bytes=62 * 2**20),
            name="mcl",
        )(init_blk, graph_blk)
        return raw * (n_all / col_sum.reshape(cols))

    return jax.shard_map(device_step, mesh=mesh, in_specs=(block_spec, block_spec), out_specs=block_spec, check_vma=False)
```

time: 549 us -> 265 us (0.48)
  waiting for transfers between devices: 410 us -> 0 us
  Pallas kernels: 0 us -> 256 us
  matrix products: 72.1 us -> 0 us
  other arithmetic: 33.8 us -> 9.18 us
  blocking collectives: 18.8 us -> 0 us
  between operations: 13.2 us -> 0.01 us
    all_gather x4 -> x0, waiting for transfers between devices: 410 us -> none  [the longest x3 305 us: device_step(): lax.all_gather(flow_blk.astype(jnp.bfloat16), 'col', axis=1, tiled=True)]
    pallas_call x0 -> x1, Pallas kernels: none -> 256 us  [device_step(): pl.pallas_call(functools.partial(kernel, float(n_all)), out_shape=(jax.Sh...]
    dot_general x3 -> x0, matrix products: 72.1 us -> none  [device_step(): jnp.dot(row_panel, graph_panel, preferred_element_type=jnp.float32)]
    convert_element_type x4 -> x0, other arithmetic: 25.2 us -> none  [the longest x3 19.2 us: device_step(): flow_blk.astype(jnp.bfloat16)]
    psum x3 -> x0, blocking collectives: 18.8 us -> none  [device_step(): col_sum = lax.psum(jnp.sum(inflated, axis=0), 'row')]
  transfers between devices with their start and end apart: 4 -> 0, of which waited for: 4 -> 0; matrix products, arithmetic and copies ran while one was open for 1% -> 0% of each run, Pallas kernels for 0% -> 0%
where the time goes in v2:
time: 265 us
  Pallas kernels  256 us (97%)
  other arithmetic  9.18 us (3%)
    pallas_call x1, Pallas kernels, device_step(): pl.pallas_call(functools.partial(kernel, float(n_all)), out_shape=(jax.Sh...  256 us
    mul x1, other arithmetic, device_step(): return raw * (n_all / col_sum.reshape(cols))  8.47 us

profile of v2, /device:TPU:0, one launch (start us, length us, event | category | flops | bytes accessed | tf_op | source)
XLA Modules:
  0.0 265.0 jit_solution(16601718409875995149)
XLA Ops:
  0.0 255.8 %mcl.1 = (f32[1024,2048]{1,0:T(8,128)}, f32[8,256]{1,0:T(8,128)}, bf16[8,4096,256]{2,1,0:T(8,128)(2,1)}) custom-call(f32[1024,2048]{1,0:T(8,128)} %flow_ref.1, f32[1024,2048]{1,0:T(8,128)} %graph_ref.1), custom_call_target="tpu_custom_call" | custom-call | tf_op jit(solution)/shard_map/mcl/pallas_call | solution.py:391
  255.8 0.7 divide_bitcast_fusion
  256.6 8.5 %broadcast_multiply_fusion = f32[1024,2048]{1,0:T(8,128)} fusion(f32[1024,2048]{1,0:T(8,128)} %get-tuple-element.7, f32[2048]{0:T(1024)S(1)} %bitcast.3), kind=kLoop, calls=%fused_computation | loop fusion | flops 2097152 | bytes 16785408 | tf_op jit(solution)/shard_map/mul | solution.py:419
  (1 shorter events, 0.0 us)

commit v3 on v2

--- a/solution.py
+++ b/solution.py
@@ -11,6 +11,7 @@
 MESH = pl.DeviceIdType.MESH
 WIDTH = 256
 PIECES = 4
+TILE_M = 512
 F32, BF16 = jnp.float32, jnp.bfloat16
 
 
@@ -26,12 +27,14 @@
 
 
 def kernel(n_all, flow_ref, graph_ref, out_ref, sum_ref, g_ref,
-           a0, a1, c1, mbuf, gown, gcol, gt, sums, s1, s2,
+           a0, a1, a2, c1, mbuf, gown, gcol, gt, sums, s1, s2,
            stage_sem, col_sem, gt_sem, out_sem,
-           xown_r, xfwd_r, ya_r, yg_r, core_r, sum_r, s1_r, s2_r,
-           xown_s, xfwd_s, ya_s, yg_s, cown_s, cfwd_s, sum_s, s1_s, s2_s):
+           xown_r, xfwd_r, ya_r, yg_r, y1_r, y2_r, core_r, sum_r, s1_r, s2_r,
+           xown_s, xfwd_s, ya_s, yg_s, y1_s, y2_s, cown_s, cfwd_s, cfar_s, sum_s, s1_s, s2_s):
     rows, cols = flow_ref.shape
     nh = cols // WIDTH
+    nf = nh - 1
+    nc = nh + nf
     depth = 4 * rows
     half = depth // 2
     quad = half // 2
@@ -94,13 +97,13 @@
             if j >= 1:
                 send_own(j - 1)
     send_own(nh - 1)
-    for j in range(nh):
+    for j in range(nf):
         for p in range(PIECES):
             src = gown.at[j, pl.ds(own + p * prow, prow)]
             dst = g_ref.at[j, pl.ds(oth + p * prow, prow)]
             remote(src, dst, yg_s, yg_r.at[j, p], yn).start()
 
-    n_pieces = nh * PIECES
+    n_pieces = nf * PIECES
 
     def relay(k, offset, sem, recv, dev, forward):
         @pl.when((k >= 0) & (k < n_pieces))
@@ -110,7 +113,7 @@
             remote(piece, piece, sem, recv.at[j, p], dev).wait_recv()
             if forward:
                 remote(piece, piece, xfwd_s, xfwd_r.at[j, p], xn).start()
-            remote(piece, piece, cfwd_s, core_r.at[nh + j], cn).start()
+            remote(piece, piece, cfar_s, core_r.at[nh + j], cn).start()
 
     def relay_y(*ks):
         for k in ks:
@@ -121,6 +124,8 @@
         for k in ks:
             with scope("relay_x"):
                 relay(jnp.int32(k), oth, xfwd_s, xfwd_r, xn, False)
+
+    lent, borrowed = pl.ds((nh - 1) * WIDTH, WIDTH), pl.ds((2 * nh - 1) * WIDTH, WIDTH)
 
     def wait_core(q):
         with scope("wait_core"):
@@ -142,6 +147,9 @@
             body(i)
             return carry
         lax.fori_loop(lo, hi, go, 0)
+
+    def over_m(body):
+        loop(0, rows // TILE_M, lambda i: body(pl.ds(pl.multiple_of(i * TILE_M, TILE_M), TILE_M)))
 
     def unrolled(n, width, body):
         def some(i):
@@ -220,11 +228,18 @@
         with scope("c0"):
             if first:
                 v = c1[q] + dot(a0[:, cols + quad:], gown[q, half + quad:, :])
+                v = v * v
+                mbuf[slot] = v
+                sums[q, r] = jnp.broadcast_to(jnp.sum(v, axis=0, keepdims=True), (8, WIDTH))
             else:
-                v = dot(a0[...], gcol[slot])
-            v = v * v
-            mbuf[slot] = v
-            sums[q, r] = jnp.broadcast_to(jnp.sum(v, axis=0, keepdims=True), (8, WIDTH))
+                sums[q, r] = jnp.zeros((8, WIDTH), F32)
+
+                def body(m):
+                    v = dot(a0[m, :], gcol[slot])
+                    v = v * v
+                    mbuf[slot, m, :] = v
+                    sums[q, r] += jnp.broadcast_to(jnp.sum(v, axis=0, keepdims=True), (8, WIDTH))
+                over_m(body)
         for dev in (cn, xn, dn):
             remote(sums.at[q, r], sums.at[q, r], sum_s, sum_r.at[q], dev).start()
 
@@ -238,7 +253,9 @@
             if first:
                 loop(0, done, lambda k: add_product(k, q, gown.at[q, k_rows(k)]))
             else:
-                c1[q] = dot(a1[:, :cols], gcol[slot, :half, :])
+                def body(m):
+                    c1[q, m, :] = dot(a1[m, :cols], gcol[slot, :half, :])
+                over_m(body)
                 loop(nh // 2, done, lambda k: add_product(k, q, gcol.at[slot, k_rows(k)]))
 
         after_left()
@@ -298,22 +315,28 @@
             relay_x(k + 4, k + 5)
 
         def after_left():
+            @pl.when(j == 0)
+            def _():
+                remote(a1.at[:, lent], a1.at[:, borrowed], y1_s, y1_r, yn).start()
             relay_y(k + 8)
             relay_x(k + 6)
         step(q, False, after_first, after_left)
         relay_y(k + 9)
         relay_x(k + 7)
 
-        @pl.when(j + 1 < nh)
+        @pl.when(j + 1 < nf)
         def _():
             wait_core(q + 1)
             col_copy(q + 1).start()
         relay_y(k + 10)
-    loop(0, nh, other_step)
+    loop(0, nf, other_step)
 
     last_kg = nh - 1
-    loop(0, nh, lambda j: tile_copy(last_kg, j).start())
-    finish(2 * nh - 1)
+    loop(0, nf, lambda j: tile_copy(last_kg, j).start())
+    s1[r] = jnp.zeros((2 * nh, WIDTH), F32)
+    finish(nc - 1)
+    with scope("wait_a1"):
+        remote(a1.at[:, lent], a1.at[:, borrowed], y1_s, y1_r, yn).wait()
 
     def close(n, g_tile):
         v = c1[n] + dot(a1[:, k_rows(last_kg)], g_tile[...])
@@ -325,8 +348,10 @@
         tile_copy(last_kg, j).wait()
         close(nh + j, gt.at[j])
     with scope("close"):
-        unrolled(nh // 4, 4, lambda n: close(n, gown.at[n, k_rows(last_kg)]))
-        unrolled(nh // 4, 4, close_other)
+        unrolled(nh // 2, 2, lambda n: close(n, gown.at[n, k_rows(last_kg)]))
+        unrolled(nf // 2, 2, close_other)
+        for j in range(nf // 2 * 2, nf):
+            close_other(j)
     for dev in (cn, xn, dn):
         remote(s1.at[r], s1.at[r], s1_s, s1_r, dev).start()
     with scope("wait_s1"):
@@ -339,25 +364,31 @@
         total = (s1[0, line, :] + s1[1, line, :]) + (s1[2, line, :] + s1[3, line, :])
         a0[:, chunk(n)] = (c1[n] * (n_all / total)).astype(BF16)
     with scope("rescale"):
-        loop(0, 2 * nh, rescale)
+        loop(nh - 1, nh + 1, rescale)
+        remote(a0.at[:, lent], a2, y2_s, y2_r, yn).start()
+        loop(0, nh - 1, rescale)
+        loop(nh + 1, nc, rescale)
+
+    near = nc * WIDTH
+
+    def last(n):
+        c1[n] = dot(a0[:, :near], gown[n, :near, :])
+    with scope("last"):
+        loop(0, nh, last)
+    with scope("wait_a2"):
+        remote(a0.at[:, lent], a2, y2_s, y2_r, yn).wait()
 
     def out_copy(n):
-        slot = lax.rem(n, 2)
-        return pltpu.make_async_copy(mbuf.at[slot], out_ref.at[:, chunk(n)], out_sem.at[slot])
-
-    def last(n):
-        slot = lax.rem(n, 2)
-
-        @pl.when(n >= 2)
-        def _():
-            out_copy(n - 2).wait()
-        v = dot(a0[...], gown[n])
+        return pltpu.make_async_copy(c1.at[n], out_ref.at[:, chunk(n)], out_sem.at[n])
+
+    def end(n):
+        v = c1[n] + dot(a2[...], gown[n, near:, :])
         v = v * v
-        mbuf[slot] = v
+        c1[n] = v
         s2[r, pl.ds(n, 1), :] = jnp.sum(v, axis=0, keepdims=True)
         out_copy(n).start()
-    with scope("last"):
-        loop(0, nh, last)
+    with scope("end"):
+        loop(0, nh, end)
 
     for dev in (cn, xn, dn):
         remote(s2.at[r], s2.at[r], s2_s, s2_r, dev).start()
@@ -365,18 +396,25 @@
     def sent(ref, sem):
         remote(ref, ref, sem, s2_r, cn).wait_send()
     sent(gown.at[:, pl.ds(0, rows)], xown_s)
-    sent(gown.at[:, pl.ds(0, rows)], yg_s)
+    sent(gown.at[pl.ds(0, nf), pl.ds(0, rows)], yg_s)
     sent(gown.at[:, pl.ds(0, rows)], cown_s)
-    sent(gown.at[:, pl.ds(0, rows)], xfwd_s)
-    sent(gown.at[:, pl.ds(0, 3 * rows)], cfwd_s)
+    sent(gown.at[pl.ds(0, nf), pl.ds(0, rows)], xfwd_s)
+    sent(gown.at[:, pl.ds(0, rows)], cfwd_s)
+    sent(gown.at[pl.ds(0, nf), pl.ds(0, 2 * rows)], cfar_s)
     sent(sums.at[:, pl.ds(0, 3)], sum_s)
     sent(s1.at[pl.ds(0, 3)], s1_s)
-    out_copy(nh - 2).wait()
-    out_copy(nh - 1).wait()
     with scope("wait_s2"):
         three = s2.at[pl.ds(0, 3)]
         remote(three, three, s2_s, s2_r, cn).wait()
-    sum_ref[...] = (s2[0] + s2[1]) + (s2[2] + s2[3])
+    total = (s2[0] + s2[1]) + (s2[2] + s2[3])
+    for n in range(nh):
+        sum_ref[:, n * WIDTH:(n + 1) * WIDTH] = total[n:n + 1]
+    with scope("wait_out"):
+        loop(0, nh, lambda n: out_copy(n).wait())
+
+
+def scale_kernel(n_all, raw_ref, sum_ref, out_ref):
+    out_ref[...] = raw_ref[...] * (n_all / sum_ref[...])
 
 
 def solution(mesh):
@@ -392,30 +430,41 @@
             functools.partial(kernel, float(n_all)),
             out_shape=(
                 jax.ShapeDtypeStruct((rows, cols), F32),
-                jax.ShapeDtypeStruct((nh, WIDTH), F32),
-                jax.ShapeDtypeStruct((nh, n_all, WIDTH), BF16),
+                jax.ShapeDtypeStruct((1, cols), F32),
+                jax.ShapeDtypeStruct((nh - 1, n_all, WIDTH), BF16),
             ),
             in_specs=[any_spec, any_spec],
             out_specs=(any_spec, pl.BlockSpec(memory_space=pltpu.VMEM), any_spec),
             scratch_shapes=[
                 pltpu.VMEM((rows, n_all), BF16),
                 pltpu.VMEM((rows, n_all), BF16),
+                pltpu.VMEM((rows, WIDTH), BF16),
                 pltpu.VMEM((2 * nh, rows, WIDTH), F32),
                 pltpu.VMEM((2, rows, WIDTH), F32),
                 pltpu.VMEM((nh, n_all, WIDTH), BF16),
                 pltpu.VMEM((2, n_all, WIDTH), BF16),
-                pltpu.VMEM((nh, 2 * WIDTH, WIDTH), BF16),
-                pltpu.VMEM((2 * nh, 4, 8, WIDTH), F32),
+                pltpu.VMEM((nh - 1, 2 * WIDTH, WIDTH), BF16),
+                pltpu.VMEM((2 * nh - 1, 4, 8, WIDTH), F32),
                 pltpu.VMEM((4, 2 * nh, WIDTH), F32),
                 pltpu.VMEM((4, nh, WIDTH), F32),
-                dma((2 * nh,)), dma((2,)), dma((nh,)), dma((2,)),
-                dma((nh,)), dma((nh, PIECES)), dma((2,)), dma((nh, PIECES)), dma((2 * nh,)), dma((2 * nh,)), dma, dma,
-                dma, dma, dma, dma, dma, dma, dma, dma, dma,
+                dma((2 * nh,)), dma((2,)), dma((nh,)), dma((nh,)),
+                dma((nh,)), dma((nh, PIECES)), dma((2,)), dma((nh, PIECES)), dma, dma,
+                dma((2 * nh,)), dma((2 * nh,)), dma, dma,
+                dma, dma, dma, dma, dma, dma, dma, dma, dma, dma, dma, dma,
             ],
             compiler_params=pltpu.CompilerParams(
                 collective_id=0, has_side_effects=True, vmem_limit_bytes=62 * 2**20),
             name="mcl",
         )(init_blk, graph_blk)
-        return raw * (n_all / col_sum.reshape(cols))
+        block = rows // 8
+        line = pl.BlockSpec((block, cols), lambda i: (i, 0))
+        return pl.pallas_call(
+            functools.partial(scale_kernel, float(n_all)),
+            out_shape=jax.ShapeDtypeStruct((rows, cols), F32),
+            grid=(8,),
+            in_specs=[line, pl.BlockSpec((1, cols), lambda i: (0, 0))],
+            out_specs=line,
+            name="scale",
+        )(raw, col_sum)
 
     return jax.shard_map(device_step, mesh=mesh, in_specs=(block_spec, block_spec), out_specs=block_spec, check_vma=False)

time: 265 us -> 252 us (0.951)
  other arithmetic: 9.18 us -> 0 us
  Pallas kernels: 256 us -> 251 us
    pallas_call x1, Pallas kernels: 256 us -> 242 us  [device_step(): pl.pallas_call(functools.partial(kernel, float(n_all)), out_shape=(jax.Sh...]
    pallas_call x0 -> x1, Pallas kernels: none -> 9 us  [device_step(): pl.pallas_call(functools.partial(scale_kernel, float(n_all)), out_shape=j...]
    mul x1 -> x0, other arithmetic: 8.47 us -> none  [device_step(): return raw * (n_all / col_sum.reshape(cols))]
where the time goes in v3:
time: 252 us; the launch traced here: 251 us
  Pallas kernels  251 us (100%)
    pallas_call x1, Pallas kernels, device_step(): pl.pallas_call(functools.partial(kernel, float(n_all)), out_shape=(jax.Sh...  242 us
    pallas_call x1, Pallas kernels, device_step(): pl.pallas_call(functools.partial(scale_kernel, float(n_all)), out_shape=j...  9 us

profile of v3, /device:TPU:0, one launch (start us, length us, event | category | flops | bytes accessed | tf_op | source)
XLA Modules:
  0.0 251.3 jit_solution(16770797450721942912)
XLA Ops:
  0.0 242.3 %mcl.1 = (f32[1024,2048]{1,0:T(8,128)}, f32[1,2048]{1,0:T(1,128)}, bf16[7,4096,256]{2,1,0:T(8,128)(2,1)}) custom-call(f32[1024,2048]{1,0:T(8,128)} %flow_ref.1, f32[1024,2048]{1,0:T(8,128)} %graph_ref.1), custom_call_target="tpu_custom_call" | custom-call | tf_op jit(solution)/shard_map/mcl/pallas_call | solution.py:429
  242.3 9.0 %scale.1 = f32[1024,2048]{1,0:T(8,128)} custom-call(f32[1024,2048]{1,0:T(8,128)} %get-tuple-element.7.raw_ref, f32[1,2048]{1,0:T(1,128)} %get-tuple-element.8.sum_ref), custom_call_target="tpu_custom_call" | custom-call | tf_op jit(solution)/shard_map/scale/pallas_call | solution.py:461

commit v4 on v3

--- a/solution.py
+++ b/solution.py
@@ -10,7 +10,7 @@
 
 MESH = pl.DeviceIdType.MESH
 WIDTH = 256
-PIECES = 4
+PIECES = 8
 TILE_M = 512
 F32, BF16 = jnp.float32, jnp.bfloat16
 
@@ -27,7 +27,7 @@
 
 
 def kernel(n_all, flow_ref, graph_ref, out_ref, sum_ref, g_ref,
-           a0, a1, a2, c1, mbuf, gown, gcol, gt, sums, s1, s2,
+           a0, a1, a2, c1, mbuf, gown, gcol, gt, sums, s1, s2, parts,
            stage_sem, col_sem, gt_sem, out_sem,
            xown_r, xfwd_r, ya_r, yg_r, y1_r, y2_r, core_r, sum_r, s1_r, s2_r,
            xown_s, xfwd_s, ya_s, yg_s, y1_s, y2_s, cown_s, cfwd_s, cfar_s, sum_s, s1_s, s2_s):
@@ -93,7 +93,8 @@
             a0[:, pl.ds(j * WIDTH, WIDTH)] = c1[nh + j].astype(BF16)
             stage(j + 3)
             if j == 1:
-                pl.semaphore_wait(bar, 4)
+                with scope('barrier'):
+                    pl.semaphore_wait(bar, 4)
             if j >= 1:
                 send_own(j - 1)
     send_own(nh - 1)
@@ -120,6 +121,9 @@
             with scope("relay_y"):
                 relay(jnp.int32(k), own, yg_s, yg_r, yn, True)
 
+    def relayed(j):
+        return PIECES * j + 13 + lax.max(0, 8 - 3 * j)
+
     def relay_x(*ks):
         for k in ks:
             with scope("relay_x"):
@@ -151,6 +155,9 @@
     def over_m(body):
         loop(0, rows // TILE_M, lambda i: body(pl.ds(pl.multiple_of(i * TILE_M, TILE_M), TILE_M)))
 
+    def fold(v):
+        return jnp.sum(v.reshape(-1, 8, WIDTH), axis=0)
+
     def unrolled(n, width, body):
         def some(i):
             for t in range(width):
@@ -192,149 +199,160 @@
                 third_quarter(first)
                 third_quarter(first + 1)
     loop(0, nh, early)
+    relay_y(0)
     with scope("early_end"):
         third_quarter(nh - 2)
         first_half(nh - 1)
         third_quarter(nh - 1)
+    relay_y(1, 2)
     wait_a(1)
 
     def add_product(kg, n, g_tile):
-        @pl.when(kg == 0)
-        def _():
-            c1[n] = dot(a1[:, k_rows(kg)], g_tile[...])
-
-        @pl.when(kg > 0)
-        def _():
-            c1[n] += dot(a1[:, k_rows(kg)], g_tile[...])
-
-    def finish(q):
+        c1[n] += dot(a1[:, k_rows(kg)], g_tile[...])
+
+    def finish(q, squares):
         with scope("finish"):
             three = sums.at[q, pl.ds(0, 3)]
             remote(three, three, sum_s, sum_r.at[q], cn).wait_recv()
             total = (sums[q, 0] + sums[q, 1]) + (sums[q, 2] + sums[q, 3])
-            scale = (n_all / total)[:1]
-            a1[:, chunk(q)] = (mbuf[lax.rem(q, 2)] * scale).astype(BF16)
-
-    def step(q, first, after_first, after_left):
-        slot = lax.rem(q, 2)
-        done = lax.div(q, 2)
-        even = slot == 0
-
-        if not first:
-            @pl.when(even)
-            def _():
-                loop(0, q - nh, lambda j: tile_copy(done - 1, j).start())
-
-        with scope("c0"):
-            if first:
-                v = c1[q] + dot(a0[:, cols + quad:], gown[q, half + quad:, :])
-                v = v * v
-                mbuf[slot] = v
-                sums[q, r] = jnp.broadcast_to(jnp.sum(v, axis=0, keepdims=True), (8, WIDTH))
-            else:
-                sums[q, r] = jnp.zeros((8, WIDTH), F32)
-
-                def body(m):
-                    v = dot(a0[m, :], gcol[slot])
-                    v = v * v
-                    mbuf[slot, m, :] = v
-                    sums[q, r] += jnp.broadcast_to(jnp.sum(v, axis=0, keepdims=True), (8, WIDTH))
-                over_m(body)
+            scale = n_all / jnp.sum(total, axis=0, keepdims=True)
+            a1[:, chunk(q)] = (squares[...] * scale).astype(BF16)
+
+    def send_sums(q):
         for dev in (cn, xn, dn):
             remote(sums.at[q, r], sums.at[q, r], sum_s, sum_r.at[q], dev).start()
 
-        after_first()
-
-        @pl.when(q >= 1)
-        def _():
-            finish(q - 1)
-
-        with scope("left"):
-            if first:
-                loop(0, done, lambda k: add_product(k, q, gown.at[q, k_rows(k)]))
-            else:
-                def body(m):
-                    c1[q, m, :] = dot(a1[m, :cols], gcol[slot, :half, :])
-                over_m(body)
-                loop(nh // 2, done, lambda k: add_product(k, q, gcol.at[slot, k_rows(k)]))
-
-        after_left()
-
-        @pl.when(even & (q >= 2))
-        def _():
-            with scope("right"):
-                kg = done - 1
-                if first:
-                    def pair(i):
-                        for n in (2 * i, 2 * i + 1):
-                            c1[n] += dot(a1[:, k_rows(kg)], gown[n, k_rows(kg), :])
-
-                    @pl.when(kg == 0)
-                    def _():
-                        for n in (0, 1):
-                            c1[n] = dot(a1[:, k_rows(0)], gown[n, k_rows(0), :])
-
-                    @pl.when(kg > 0)
-                    def _():
-                        loop(0, done, pair)
-                else:
-                    def some(i):
-                        for n in range(4):
-                            c1[4 * i + n] += dot(a1[:, k_rows(kg)], gown[4 * i + n, k_rows(kg), :])
-                    loop(0, nh // 4, some)
-
-                    def pair(i):
-                        for j in (2 * i, 2 * i + 1):
-                            tile_copy(kg, j).wait()
-                        for j in (2 * i, 2 * i + 1):
-                            c1[nh + j] += dot(a1[:, k_rows(kg)], gt[j])
-                    loop(0, done - nh // 2, pair)
-
-    def own_step(q):
-        def after_first():
-            for at, ys, xs in ((1, (0,), ()), (2, (1,), ()), (4, (2,), ()), (5, (3,), (0, 1)), (6, (4,), ()), (7, (5,), (2,))):
-                @pl.when(q == at)
-                def _():
-                    relay_y(*ys)
-                    relay_x(*xs)
-        step(q, True, after_first, lambda: None)
-    loop(0, nh, own_step)
-    relay_y(6)
-    relay_x(3)
-    wait_core(nh)
-    col_copy(nh).start()
+    def own_expand(q):
+        with scope("c0"):
+            v = c1[q] + dot(a0[:, cols + quad:], gown[q, half + quad:, :])
+            v = v * v
+            c1[q] = v
+            sums[q, r] = fold(v)
+        send_sums(q)
+        for at, k in ((0, 3), (2, 4), (3, 5), (5, 6), (7, 7)):
+            @pl.when(q == at)
+            def _():
+                relay_y(k)
+    loop(0, nh, own_expand)
+
+    def own_finish(q):
+        finish(q, c1.at[q])
+        for at, k in ((2, 8), (3, 9), (5, 10), (7, 11)):
+            @pl.when(q == at)
+            def _():
+                relay_y(k)
+    loop(0, nh, own_finish)
+    relay_x(0, 1, 2, 3, 4, 5, 6, 7)
+    relay_y(12)
+    remote(a1.at[:, lent], a1.at[:, borrowed], y1_s, y1_r, yn).start()
+
+    def own_products(n):
+        with scope("own_products"):
+            c1[n] = dot(a1[:, :cols], gown[n, :half, :])
+        relay_y(13 + n)
+
+        @pl.when(n == 2)
+        def _():
+            wait_core(nh)
+            col_copy(nh).start()
+    loop(0, nh, own_products)
+
+    def right_own(kg):
+        def some(i):
+            for n in range(4):
+                c1[4 * i + n] += dot(a1[:, k_rows(kg)], gown[4 * i + n, k_rows(kg), :])
+        with scope("right_own"):
+            loop(0, nh // 4, some)
+
+    def right_other(kg, pairs):
+        def pair(i):
+            for j in (2 * i, 2 * i + 1):
+                tile_copy(kg, j).wait()
+            for j in (2 * i, 2 * i + 1):
+                c1[nh + j] += dot(a1[:, k_rows(kg)], gt[j])
+        with scope("right_other"):
+            loop(0, pairs, pair)
 
     def other_step(j):
         q = nh + j
         k = PIECES * j
+        slot = lax.rem(q, 2)
+        done = lax.div(q, 2)
+        at_last = j == nf - 2
+        paired = ((slot == 0) & (j > 0) & (j < nf - 1)) | at_last
+        kg = lax.div(q - 1, 2)
+        pairs = lax.div(j + 1, 2)
+        ahead = relayed(j)
+
+        def relay_ahead(*steps):
+            for i in steps:
+                @pl.when(ahead + i < relayed(j + 1))
+                def _():
+                    relay_y(ahead + i)
+
+        def relay_next(*steps):
+            for i in steps:
+                relay_x(k + PIECES + i)
         with scope("load"):
             col_copy(q).wait()
 
-        def after_first():
-            relay_y(k + 7)
-            relay_x(k + 4, k + 5)
-
-        def after_left():
-            @pl.when(j == 0)
-            def _():
-                remote(a1.at[:, lent], a1.at[:, borrowed], y1_s, y1_r, yn).start()
-            relay_y(k + 8)
-            relay_x(k + 6)
-        step(q, False, after_first, after_left)
-        relay_y(k + 9)
-        relay_x(k + 7)
+        @pl.when(paired)
+        def _():
+            loop(0, 2 * pairs, lambda i: tile_copy(kg, i).start())
+        relay_ahead(0)
+        sums[q, r] = jnp.zeros((8, WIDTH), F32)
+
+        def expand(m):
+            v = dot(a0[m, :], gcol[slot])
+            v = v * v
+            mbuf[slot, m, :] = v
+            sums[q, r] += fold(v)
+        with scope("c0"):
+            over_m(expand)
+        send_sums(q)
+        relay_ahead(1, 2)
+        relay_next(0, 1, 2)
+
+        @pl.when((j > 0) & (j < nf - 1))
+        def _():
+            finish(q - 1, mbuf.at[1 - slot])
+
+        def expand_flow(m):
+            c1[q, m, :] = dot(a1[m, :cols], gcol[slot, :half, :])
+        with scope("left"):
+            over_m(expand_flow)
+            loop(nh // 2, done, lambda i: add_product(i, q, gcol.at[slot, k_rows(i)]))
+        relay_ahead(3)
+        relay_next(3, 4)
+
+        @pl.when(at_last)
+        def _():
+            finish(q, mbuf.at[slot])
+
+        @pl.when(paired)
+        def _():
+            right_own(kg)
+        relay_next(5)
+        relay_ahead(4)
+        relay_next(6)
+        relay_ahead(5)
+        relay_next(7)
 
         @pl.when(j + 1 < nf)
         def _():
             wait_core(q + 1)
             col_copy(q + 1).start()
-        relay_y(k + 10)
+
+        @pl.when(paired)
+        def _():
+            right_other(kg, pairs)
+        relay_ahead(6, 7)
     loop(0, nf, other_step)
 
     last_kg = nh - 1
     loop(0, nf, lambda j: tile_copy(last_kg, j).start())
-    s1[r] = jnp.zeros((2 * nh, WIDTH), F32)
-    finish(nc - 1)
+    parts[2 * nh - 1] = jnp.zeros((8, WIDTH), F32)
+    finish(nc - 1, mbuf.at[(nc - 1) % 2])
     with scope("wait_a1"):
         remote(a1.at[:, lent], a1.at[:, borrowed], y1_s, y1_r, yn).wait()
 
@@ -342,53 +360,86 @@
         v = c1[n] + dot(a1[:, k_rows(last_kg)], g_tile[...])
         v = v * v
         c1[n] = v
-        s1[r, pl.ds(n, 1), :] = jnp.sum(v, axis=0, keepdims=True)
+        parts[n] = fold(v)
 
     def close_other(j):
         tile_copy(last_kg, j).wait()
         close(nh + j, gt.at[j])
+    def send_s1(i):
+        part = s1.at[i, r]
+        for dev in (cn, xn, dn):
+            remote(part, part, s1_s, s1_r.at[i], dev).start()
+
     with scope("close"):
-        unrolled(nh // 2, 2, lambda n: close(n, gown.at[n, k_rows(last_kg)]))
+        unrolled(nh // 4, 4, lambda n: close(n, gown.at[n, k_rows(last_kg)]))
+        s1[0, r] = jnp.sum(parts[:nh], axis=1)
+    send_s1(0)
+    with scope("close"):
         unrolled(nf // 2, 2, close_other)
         for j in range(nf // 2 * 2, nf):
             close_other(j)
-    for dev in (cn, xn, dn):
-        remote(s1.at[r], s1.at[r], s1_s, s1_r, dev).start()
-    with scope("wait_s1"):
-        remote(a0.at[:, pl.ds(0, cols)], a0.at[:, pl.ds(0, cols)], ya_s, ya_r.at[0], yn).wait_send()
-        three = s1.at[pl.ds(0, 3)]
-        remote(three, three, s1_s, s1_r, cn).wait_recv()
-
-    def rescale(n):
+        s1[1, r] = jnp.sum(parts[nh:], axis=1)
+    send_s1(1)
+
+    def wait_s1(i):
+        with scope("wait_s1"):
+            three = s1.at[i, pl.ds(0, 3)]
+            remote(three, three, s1_s, s1_r.at[i], cn).wait_recv()
+
+    def rescale(i, n):
         line = pl.ds(n, 1)
-        total = (s1[0, line, :] + s1[1, line, :]) + (s1[2, line, :] + s1[3, line, :])
-        a0[:, chunk(n)] = (c1[n] * (n_all / total)).astype(BF16)
+        total = (s1[i, 0, line, :] + s1[i, 1, line, :]) + (s1[i, 2, line, :] + s1[i, 3, line, :])
+        a0[:, chunk(i * nh + n)] = (c1[i * nh + n] * (n_all / total)).astype(BF16)
+
+    remote(a0.at[:, pl.ds(0, cols)], a0.at[:, pl.ds(0, cols)], ya_s, ya_r.at[0], yn).wait_send()
+    wait_s1(0)
     with scope("rescale"):
-        loop(nh - 1, nh + 1, rescale)
-        remote(a0.at[:, lent], a2, y2_s, y2_r, yn).start()
-        loop(0, nh - 1, rescale)
-        loop(nh + 1, nc, rescale)
+        loop(0, nh, lambda i: rescale(0, nh - 1 - i))
 
     near = nc * WIDTH
+
+    def out_copy(n):
+        return pltpu.make_async_copy(c1.at[n], out_ref.at[:, chunk(n)], out_sem.at[n])
+
+    def put(n, v):
+        v = v * v
+        c1[n] = v
+        parts[n] = fold(v)
+
+    def last_near(n):
+        c1[n] = dot(a0[:, :cols], gown[n, :half, :])
+
+    def last_other(n):
+        c1[n] += dot(a0[:, cols:near], gown[n, half:near, :])
 
     def last(n):
         c1[n] = dot(a0[:, :near], gown[n, :near, :])
+
+    def last_far(i):
+        put(2 * i, c1[2 * i] + dot(a2[...], gown[2 * i, near:, :]))
+        put(2 * i + 1, c1[2 * i + 1] + dot(a2[...], gown[2 * i + 1, near:, :]))
+        out_copy(2 * i).start()
+        out_copy(2 * i + 1).start()
+
+    def last_whole(n):
+        put(n, dot(a0[:, :near], gown[n, :near, :]) + dot(a2[...], gown[n, near:, :]))
+        out_copy(n).start()
+    with scope("last_near"):
+        remote(a0.at[:, lent], a2, y2_s, y2_r, yn).start()
+        loop(0, 2, last_near)
+    wait_s1(1)
+    with scope("rescale"):
+        loop(0, nf, lambda n: rescale(1, n))
     with scope("last"):
-        loop(0, nh, last)
+        loop(0, 2, last_other)
+        loop(2, nh - 2, last)
     with scope("wait_a2"):
         remote(a0.at[:, lent], a2, y2_s, y2_r, yn).wait()
-
-    def out_copy(n):
-        return pltpu.make_async_copy(c1.at[n], out_ref.at[:, chunk(n)], out_sem.at[n])
-
-    def end(n):
-        v = c1[n] + dot(a2[...], gown[n, near:, :])
-        v = v * v
-        c1[n] = v
-        s2[r, pl.ds(n, 1), :] = jnp.sum(v, axis=0, keepdims=True)
-        out_copy(n).start()
-    with scope("end"):
-        loop(0, nh, end)
+    with scope("last_far"):
+        loop(0, (nh - 2) // 2, last_far)
+    with scope("last_whole"):
+        loop(nh - 2, nh, last_whole)
+        s2[r] = jnp.sum(parts[:nh], axis=1)
 
     for dev in (cn, xn, dn):
         remote(s2.at[r], s2.at[r], s2_s, s2_r, dev).start()
@@ -402,7 +453,7 @@
     sent(gown.at[:, pl.ds(0, rows)], cfwd_s)
     sent(gown.at[pl.ds(0, nf), pl.ds(0, 2 * rows)], cfar_s)
     sent(sums.at[:, pl.ds(0, 3)], sum_s)
-    sent(s1.at[pl.ds(0, 3)], s1_s)
+    sent(s1.at[:, pl.ds(0, 3)], s1_s)
     with scope("wait_s2"):
         three = s2.at[pl.ds(0, 3)]
         remote(three, three, s2_s, s2_r, cn).wait()
@@ -413,8 +464,27 @@
         loop(0, nh, lambda n: out_copy(n).wait())
 
 
-def scale_kernel(n_all, raw_ref, sum_ref, out_ref):
-    out_ref[...] = raw_ref[...] * (n_all / sum_ref[...])
+BLOCKS = 8
+
+
+def scale_kernel(n_all, raw_ref, sum_ref, out_ref, buf, in_sem, out_sem):
+    rows = buf.shape[1]
+
+    def get(i):
+        return pltpu.make_async_copy(raw_ref.at[pl.ds(i * rows, rows)], buf.at[i], in_sem.at[i])
+
+    def put(i):
+        return pltpu.make_async_copy(buf.at[i], out_ref.at[pl.ds(i * rows, rows)], out_sem.at[i])
+
+    for i in range(BLOCKS):
+        get(i).start()
+    scale = n_all / sum_ref[...]
+    for i in range(BLOCKS):
+        get(i).wait()
+        buf[i] = buf[i] * scale
+        put(i).start()
+    for i in range(BLOCKS):
+        put(i).wait()
 
 
 def solution(mesh):
@@ -445,25 +515,26 @@
                 pltpu.VMEM((2, n_all, WIDTH), BF16),
                 pltpu.VMEM((nh - 1, 2 * WIDTH, WIDTH), BF16),
                 pltpu.VMEM((2 * nh - 1, 4, 8, WIDTH), F32),
-                pltpu.VMEM((4, 2 * nh, WIDTH), F32),
+                pltpu.VMEM((2, 4, nh, WIDTH), F32),
                 pltpu.VMEM((4, nh, WIDTH), F32),
+                pltpu.VMEM((2 * nh, 8, WIDTH), F32),
                 dma((2 * nh,)), dma((2,)), dma((nh,)), dma((nh,)),
                 dma((nh,)), dma((nh, PIECES)), dma((2,)), dma((nh, PIECES)), dma, dma,
-                dma((2 * nh,)), dma((2 * nh,)), dma, dma,
+                dma((2 * nh,)), dma((2 * nh,)), dma((2,)), dma,
                 dma, dma, dma, dma, dma, dma, dma, dma, dma, dma, dma, dma,
             ],
             compiler_params=pltpu.CompilerParams(
                 collective_id=0, has_side_effects=True, vmem_limit_bytes=62 * 2**20),
             name="mcl",
         )(init_blk, graph_blk)
-        block = rows // 8
-        line = pl.BlockSpec((block, cols), lambda i: (i, 0))
+        dma_blocks = dma((BLOCKS,))
         return pl.pallas_call(
             functools.partial(scale_kernel, float(n_all)),
             out_shape=jax.ShapeDtypeStruct((rows, cols), F32),
-            grid=(8,),
-            in_specs=[line, pl.BlockSpec((1, cols), lambda i: (0, 0))],
-            out_specs=line,
+            in_specs=[any_spec, pl.BlockSpec(memory_space=pltpu.VMEM)],
+            out_specs=any_spec,
+            scratch_shapes=[pltpu.VMEM((BLOCKS, rows // BLOCKS, cols), F32), dma_blocks, dma_blocks],
+            compiler_params=pltpu.CompilerParams(vmem_limit_bytes=62 * 2**20),
             name="scale",
         )(raw, col_sum)
 

time: 252 us -> 236 us (0.937)
  Pallas kernels: 251 us -> 236 us
    pallas_call x1, Pallas kernels: 242 us -> 229 us  [device_step(): pl.pallas_call(functools.partial(kernel, float(n_all)), out_shape=(jax.Sh...]
where the time goes in v4:
time: 236 us
  Pallas kernels  236 us (100%)
    pallas_call x1, Pallas kernels, device_step(): pl.pallas_call(functools.partial(kernel, float(n_all)), out_shape=(jax.Sh...  229 us
    pallas_call x1, Pallas kernels, device_step(): pl.pallas_call(functools.partial(scale_kernel, float(n_all)), out_shape=j...  7.26 us

profile of v4, /device:TPU:0, one launch (start us, length us, event | category | flops | bytes accessed | tf_op | source)
XLA Modules:
  0.0 236.0 jit_solution(13289227152651788913)
XLA Ops:
  0.0 228.6 %mcl.1 = (f32[1024,2048]{1,0:T(8,128)}, f32[1,2048]{1,0:T(1,128)}, bf16[7,4096,256]{2,1,0:T(8,128)(2,1)}) custom-call(f32[1024,2048]{1,0:T(8,128)} %flow_ref.1, f32[1024,2048]{1,0:T(8,128)} %graph_ref.1), custom_call_target="tpu_custom_call" | custom-call | tf_op jit(solution)/shard_map/mcl/pallas_call | solution.py:499
  228.6 7.3 %scale.1 = f32[1024,2048]{1,0:T(8,128)} custom-call(f32[1024,2048]{1,0:T(8,128)} %get-tuple-element.7.raw_ref, f32[1,2048]{1,0:T(1,128)} %get-tuple-element.8.sum_ref), custom_call_target="tpu_custom_call" | custom-call | tf_op jit(solution)/shard_map/scale/pallas_call | solution.py:531

commit v5 on v4

--- a/solution.py
+++ b/solution.py
@@ -26,9 +26,9 @@
     return jnp.dot(a, b, preferred_element_type=F32)
 
 
-def kernel(n_all, flow_ref, graph_ref, out_ref, sum_ref, g_ref,
-           a0, a1, a2, c1, mbuf, gown, gcol, gt, sums, s1, s2, parts,
-           stage_sem, col_sem, gt_sem, out_sem,
+def kernel(n_all, flow_ref, graph_ref, c1, sum_ref, g_ref,
+           a0, a1, a2, c1o, mbuf, gown, gcol, gt, sums, s1, s2, parts,
+           stage_sem, col_sem, gt_sem,
            xown_r, xfwd_r, ya_r, yg_r, y1_r, y2_r, core_r, sum_r, s1_r, s2_r,
            xown_s, xfwd_s, ya_s, yg_s, y1_s, y2_s, cown_s, cfwd_s, cfar_s, sum_s, s1_s, s2_s):
     rows, cols = flow_ref.shape
@@ -64,13 +64,15 @@
 
     def stage_copy(k):
         src = graph_ref if k < nh else flow_ref
-        return pltpu.make_async_copy(src.at[:, pl.ds((k % nh) * WIDTH, WIDTH)], c1.at[k], stage_sem.at[k])
+        return pltpu.make_async_copy(src.at[:, pl.ds((k % nh) * WIDTH, WIDTH)],
+                                     c1.at[k] if k < nh else c1o.at[k - nh], stage_sem.at[k])
 
     def stage(j):
         if j < nh:
             stage_copy(j).start()
             stage_copy(nh + j).start()
 
+    gt[nh - 1] = jnp.zeros((kg_rows, WIDTH), BF16)
     stage(0)
     bar = pltpu.get_barrier_semaphore()
     for dev in (xn, yn, cn, dn):
@@ -90,7 +92,7 @@
             stage_copy(j).wait()
             gown[j, mine, :] = c1[j].astype(BF16)
             stage_copy(nh + j).wait()
-            a0[:, pl.ds(j * WIDTH, WIDTH)] = c1[nh + j].astype(BF16)
+            a0[:, pl.ds(j * WIDTH, WIDTH)] = c1o[j].astype(BF16)
             stage(j + 3)
             if j == 1:
                 with scope('barrier'):
@@ -122,7 +124,7 @@
                 relay(jnp.int32(k), own, yg_s, yg_r, yn, True)
 
     def relayed(j):
-        return PIECES * j + 13 + lax.max(0, 8 - 3 * j)
+        return PIECES * j + 13 + lax.max(0, 6 - 4 * j)
 
     def relay_x(*ks):
         for k in ks:
@@ -207,8 +209,8 @@
     relay_y(1, 2)
     wait_a(1)
 
-    def add_product(kg, n, g_tile):
-        c1[n] += dot(a1[:, k_rows(kg)], g_tile[...])
+    def add_other(kg, j, g_tile):
+        c1o[j] += dot(a1[:, k_rows(kg)], g_tile[...])
 
     def finish(q, squares):
         with scope("finish"):
@@ -235,27 +237,39 @@
                 relay_y(k)
     loop(0, nh, own_expand)
 
+    def after(i, *relays):
+        for at, k in relays:
+            @pl.when(i == at)
+            def _():
+                relay_y(k)
+
     def own_finish(q):
         finish(q, c1.at[q])
-        for at, k in ((2, 8), (3, 9), (5, 10), (7, 11)):
-            @pl.when(q == at)
-            def _():
-                relay_y(k)
-    loop(0, nh, own_finish)
+        after(q, (1, 8), (3, 9), (7, 12))
+
+    def own_first(n):
+        with scope("own_first"):
+            c1[n] = dot(a1[:, :quad], gown[n, :quad, :])
+        after(n, (0, 10), (2, 11))
+
+    def own_second(n):
+        with scope("own_second"):
+            c1[n] += dot(a1[:, quad:cols], gown[n, quad:half, :])
+        after(n, (1, 13), (3, 14))
+
+    def own_whole(n):
+        with scope("own_whole"):
+            c1[n] = dot(a1[:, :cols], gown[n, :half, :])
+        relay_y(15 - nh // 2 + n)
+    loop(0, nh // 2, own_finish)
+    loop(0, nh // 2, own_first)
+    loop(nh // 2, nh, own_finish)
     relay_x(0, 1, 2, 3, 4, 5, 6, 7)
-    relay_y(12)
+    loop(0, nh // 2, own_second)
     remote(a1.at[:, lent], a1.at[:, borrowed], y1_s, y1_r, yn).start()
-
-    def own_products(n):
-        with scope("own_products"):
-            c1[n] = dot(a1[:, :cols], gown[n, :half, :])
-        relay_y(13 + n)
-
-        @pl.when(n == 2)
-        def _():
-            wait_core(nh)
-            col_copy(nh).start()
-    loop(0, nh, own_products)
+    wait_core(nh)
+    col_copy(nh).start()
+    loop(nh // 2, nh, own_whole)
 
     def right_own(kg):
         def some(i):
@@ -264,12 +278,21 @@
         with scope("right_own"):
             loop(0, nh // 4, some)
 
+    def right_one(q):
+        k_one = chunk(q)
+
+        def some(i):
+            for n in range(4):
+                c1[4 * i + n] += dot(a1[:, k_one], gown[4 * i + n, k_one, :])
+        with scope("right_one"):
+            loop(0, nh // 4, some)
+
     def right_other(kg, pairs):
         def pair(i):
             for j in (2 * i, 2 * i + 1):
                 tile_copy(kg, j).wait()
             for j in (2 * i, 2 * i + 1):
-                c1[nh + j] += dot(a1[:, k_rows(kg)], gt[j])
+                add_other(kg, j, gt.at[j])
         with scope("right_other"):
             loop(0, pairs, pair)
 
@@ -318,18 +341,20 @@
             finish(q - 1, mbuf.at[1 - slot])
 
         def expand_flow(m):
-            c1[q, m, :] = dot(a1[m, :cols], gcol[slot, :half, :])
+            c1o[j, m, :] = dot(a1[m, :cols], gcol[slot, :half, :])
         with scope("left"):
             over_m(expand_flow)
-            loop(nh // 2, done, lambda i: add_product(i, q, gcol.at[slot, k_rows(i)]))
+            loop(nh // 2, done, lambda i: add_other(i, j, gcol.at[slot, k_rows(i)]))
         relay_ahead(3)
         relay_next(3, 4)
 
         @pl.when(at_last)
         def _():
+            right_one(q - 1)
             finish(q, mbuf.at[slot])
-
-        @pl.when(paired)
+            right_one(q)
+
+        @pl.when(paired & ~at_last)
         def _():
             right_own(kg)
         relay_next(5)
@@ -351,33 +376,31 @@
 
     last_kg = nh - 1
     loop(0, nf, lambda j: tile_copy(last_kg, j).start())
-    parts[2 * nh - 1] = jnp.zeros((8, WIDTH), F32)
     finish(nc - 1, mbuf.at[(nc - 1) % 2])
     with scope("wait_a1"):
         remote(a1.at[:, lent], a1.at[:, borrowed], y1_s, y1_r, yn).wait()
 
-    def close(n, g_tile):
-        v = c1[n] + dot(a1[:, k_rows(last_kg)], g_tile[...])
+    def close(c, i, part, g_tile):
+        v = c[i] + dot(a1[:, k_rows(last_kg)], g_tile[...])
         v = v * v
-        c1[n] = v
-        parts[n] = fold(v)
+        c[i] = v
+        parts[part] = fold(v)
 
     def close_other(j):
-        tile_copy(last_kg, j).wait()
-        close(nh + j, gt.at[j])
+        close(c1o, j, nh + j, gt.at[j])
+
     def send_s1(i):
         part = s1.at[i, r]
         for dev in (cn, xn, dn):
             remote(part, part, s1_s, s1_r.at[i], dev).start()
 
     with scope("close"):
-        unrolled(nh // 4, 4, lambda n: close(n, gown.at[n, k_rows(last_kg)]))
+        unrolled(nh // 4, 4, lambda n: close(c1, n, n, gown.at[n, k_rows(last_kg)]))
         s1[0, r] = jnp.sum(parts[:nh], axis=1)
     send_s1(0)
     with scope("close"):
-        unrolled(nf // 2, 2, close_other)
-        for j in range(nf // 2 * 2, nf):
-            close_other(j)
+        loop(0, nf, lambda j: tile_copy(last_kg, j).wait())
+        unrolled(nh // 4, 4, close_other)
         s1[1, r] = jnp.sum(parts[nh:], axis=1)
     send_s1(1)
 
@@ -389,7 +412,7 @@
     def rescale(i, n):
         line = pl.ds(n, 1)
         total = (s1[i, 0, line, :] + s1[i, 1, line, :]) + (s1[i, 2, line, :] + s1[i, 3, line, :])
-        a0[:, chunk(i * nh + n)] = (c1[i * nh + n] * (n_all / total)).astype(BF16)
+        a0[:, chunk(i * nh + n)] = ((c1 if i == 0 else c1o)[n] * (n_all / total)).astype(BF16)
 
     remote(a0.at[:, pl.ds(0, cols)], a0.at[:, pl.ds(0, cols)], ya_s, ya_r.at[0], yn).wait_send()
     wait_s1(0)
@@ -398,9 +421,6 @@
 
     near = nc * WIDTH
 
-    def out_copy(n):
-        return pltpu.make_async_copy(c1.at[n], out_ref.at[:, chunk(n)], out_sem.at[n])
-
     def put(n, v):
         v = v * v
         c1[n] = v
@@ -418,12 +438,9 @@
     def last_far(i):
         put(2 * i, c1[2 * i] + dot(a2[...], gown[2 * i, near:, :]))
         put(2 * i + 1, c1[2 * i + 1] + dot(a2[...], gown[2 * i + 1, near:, :]))
-        out_copy(2 * i).start()
-        out_copy(2 * i + 1).start()
 
     def last_whole(n):
         put(n, dot(a0[:, :near], gown[n, :near, :]) + dot(a2[...], gown[n, near:, :]))
-        out_copy(n).start()
     with scope("last_near"):
         remote(a0.at[:, lent], a2, y2_s, y2_r, yn).start()
         loop(0, 2, last_near)
@@ -460,30 +477,17 @@
     total = (s2[0] + s2[1]) + (s2[2] + s2[3])
     for n in range(nh):
         sum_ref[:, n * WIDTH:(n + 1) * WIDTH] = total[n:n + 1]
-    with scope("wait_out"):
-        loop(0, nh, lambda n: out_copy(n).wait())
-
-
-BLOCKS = 8
-
-
-def scale_kernel(n_all, raw_ref, sum_ref, out_ref, buf, in_sem, out_sem):
-    rows = buf.shape[1]
-
-    def get(i):
-        return pltpu.make_async_copy(raw_ref.at[pl.ds(i * rows, rows)], buf.at[i], in_sem.at[i])
-
+
+
+def scale_kernel(n_all, raw_ref, sum_ref, out_ref, buf, out_sem):
     def put(i):
-        return pltpu.make_async_copy(buf.at[i], out_ref.at[pl.ds(i * rows, rows)], out_sem.at[i])
-
-    for i in range(BLOCKS):
-        get(i).start()
-    scale = n_all / sum_ref[...]
-    for i in range(BLOCKS):
-        get(i).wait()
-        buf[i] = buf[i] * scale
+        return pltpu.make_async_copy(buf.at[i], out_ref.at[:, pl.ds(i * WIDTH, WIDTH)], out_sem.at[i])
+
+    chunks = raw_ref.shape[0]
+    for i in range(chunks):
+        buf[i] = raw_ref[i] * (n_all / sum_ref[:, i * WIDTH:(i + 1) * WIDTH])
         put(i).start()
-    for i in range(BLOCKS):
+    for i in range(chunks):
         put(i).wait()
 
 
@@ -495,46 +499,45 @@
         n_all = 2 * cols
         nh = cols // WIDTH
         dma = pltpu.SemaphoreType.DMA
-        any_spec = pl.BlockSpec(memory_space=pl.ANY)
+        any_spec, vmem_spec = pl.BlockSpec(memory_space=pl.ANY), pl.BlockSpec(memory_space=pltpu.VMEM)
         raw, col_sum, _ = pl.pallas_call(
             functools.partial(kernel, float(n_all)),
             out_shape=(
-                jax.ShapeDtypeStruct((rows, cols), F32),
-                jax.ShapeDtypeStruct((1, cols), F32),
+                pltpu.VMEM((nh, rows, WIDTH), F32),
+                pltpu.VMEM((1, cols), F32),
                 jax.ShapeDtypeStruct((nh - 1, n_all, WIDTH), BF16),
             ),
             in_specs=[any_spec, any_spec],
-            out_specs=(any_spec, pl.BlockSpec(memory_space=pltpu.VMEM), any_spec),
+            out_specs=(vmem_spec, vmem_spec, any_spec),
             scratch_shapes=[
                 pltpu.VMEM((rows, n_all), BF16),
                 pltpu.VMEM((rows, n_all), BF16),
                 pltpu.VMEM((rows, WIDTH), BF16),
-                pltpu.VMEM((2 * nh, rows, WIDTH), F32),
+                pltpu.VMEM((nh, rows, WIDTH), F32),
                 pltpu.VMEM((2, rows, WIDTH), F32),
                 pltpu.VMEM((nh, n_all, WIDTH), BF16),
                 pltpu.VMEM((2, n_all, WIDTH), BF16),
-                pltpu.VMEM((nh - 1, 2 * WIDTH, WIDTH), BF16),
+                pltpu.VMEM((nh, 2 * WIDTH, WIDTH), BF16),
                 pltpu.VMEM((2 * nh - 1, 4, 8, WIDTH), F32),
                 pltpu.VMEM((2, 4, nh, WIDTH), F32),
                 pltpu.VMEM((4, nh, WIDTH), F32),
                 pltpu.VMEM((2 * nh, 8, WIDTH), F32),
-                dma((2 * nh,)), dma((2,)), dma((nh,)), dma((nh,)),
+                dma((2 * nh,)), dma((2,)), dma((nh,)),
                 dma((nh,)), dma((nh, PIECES)), dma((2,)), dma((nh, PIECES)), dma, dma,
                 dma((2 * nh,)), dma((2 * nh,)), dma((2,)), dma,
                 dma, dma, dma, dma, dma, dma, dma, dma, dma, dma, dma, dma,
             ],
             compiler_params=pltpu.CompilerParams(
-                collective_id=0, has_side_effects=True, vmem_limit_bytes=62 * 2**20),
+                collective_id=0, has_side_effects=True, vmem_limit_bytes=54 * 2**20),
             name="mcl",
         )(init_blk, graph_blk)
-        dma_blocks = dma((BLOCKS,))
         return pl.pallas_call(
             functools.partial(scale_kernel, float(n_all)),
             out_shape=jax.ShapeDtypeStruct((rows, cols), F32),
-            in_specs=[any_spec, pl.BlockSpec(memory_space=pltpu.VMEM)],
+            in_specs=[vmem_spec, vmem_spec],
             out_specs=any_spec,
-            scratch_shapes=[pltpu.VMEM((BLOCKS, rows // BLOCKS, cols), F32), dma_blocks, dma_blocks],
-            compiler_params=pltpu.CompilerParams(vmem_limit_bytes=62 * 2**20),
+            scratch_shapes=[pltpu.VMEM((nh, rows, WIDTH), F32), dma((nh,))],
+            compiler_params=pltpu.CompilerParams(vmem_limit_bytes=40 * 2**20),
             name="scale",
         )(raw, col_sum)
 

time: 236 us -> 230 us (0.975)
  Pallas kernels: 236 us -> 229 us
    pallas_call x1, Pallas kernels: 7.26 us -> 3.44 us  [device_step(): pl.pallas_call(functools.partial(scale_kernel, float(n_all)), out_shape=j...]
    pallas_call x1, Pallas kernels: 229 us -> 226 us  [device_step(): pl.pallas_call(functools.partial(kernel, float(n_all)), out_shape=(pltpu....]
where the time goes in v5:
time: 230 us
  Pallas kernels  229 us (100%)
    pallas_call x1, Pallas kernels, device_step(): pl.pallas_call(functools.partial(kernel, float(n_all)), out_shape=(pltpu....  226 us

profile of v5, /device:TPU:0, one launch (start us, length us, event | category | flops | bytes accessed | tf_op | source)
XLA Modules:
  0.0 229.6 jit_solution(4246274541237278962)
XLA Ops:
  0.0 226.0 %mcl.1 = (f32[8,1024,256]{2,1,0:T(8,128)S(1)}, f32[1,2048]{1,0:T(1,128)S(1)}, bf16[7,4096,256]{2,1,0:T(8,128)(2,1)}) custom-call(f32[1024,2048]{1,0:T(8,128)} %flow_ref.1, f32[1024,2048]{1,0:T(8,128)} %graph_ref.1), custom_call_target="tpu_custom_call" | custom-call | tf_op jit(solution)/shard_map/mcl/pallas_call | solution.py:503
  226.0 3.4 %scale.1 = f32[1024,2048]{1,0:T(8,128)} custom-call(f32[8,1024,256]{2,1,0:T(8,128)S(1)} %get-tuple-element.7.raw_ref, f32[1,2048]{1,0:T(1,128)S(1)} %get-tuple-element.8.sum_ref), custom_call_target="tpu_custom_call" | custom-call | tf_op jit(solution)/shard_map/scale/pallas_call | solution.py:534

commit v6 on v5

--- a/solution.py
+++ b/solution.py
@@ -217,7 +217,7 @@
             three = sums.at[q, pl.ds(0, 3)]
             remote(three, three, sum_s, sum_r.at[q], cn).wait_recv()
             total = (sums[q, 0] + sums[q, 1]) + (sums[q, 2] + sums[q, 3])
-            scale = n_all / jnp.sum(total, axis=0, keepdims=True)
+            scale = n_all / total
             a1[:, chunk(q)] = (squares[...] * scale).astype(BF16)
 
     def send_sums(q):
@@ -229,7 +229,7 @@
             v = c1[q] + dot(a0[:, cols + quad:], gown[q, half + quad:, :])
             v = v * v
             c1[q] = v
-            sums[q, r] = fold(v)
+            sums[q, r] = jnp.sum(fold(v), axis=0, keepdims=True)
         send_sums(q)
         for at, k in ((0, 3), (2, 4), (3, 5), (5, 6), (7, 7)):
             @pl.when(q == at)
@@ -323,13 +323,13 @@
         def _():
             loop(0, 2 * pairs, lambda i: tile_copy(kg, i).start())
         relay_ahead(0)
-        sums[q, r] = jnp.zeros((8, WIDTH), F32)
+        sums[q, r] = jnp.zeros((1, WIDTH), F32)
 
         def expand(m):
             v = dot(a0[m, :], gcol[slot])
             v = v * v
             mbuf[slot, m, :] = v
-            sums[q, r] += fold(v)
+            sums[q, r] += jnp.sum(fold(v), axis=0, keepdims=True)
         with scope("c0"):
             over_m(expand)
         send_sums(q)
@@ -518,7 +518,7 @@
                 pltpu.VMEM((nh, n_all, WIDTH), BF16),
                 pltpu.VMEM((2, n_all, WIDTH), BF16),
                 pltpu.VMEM((nh, 2 * WIDTH, WIDTH), BF16),
-                pltpu.VMEM((2 * nh - 1, 4, 8, WIDTH), F32),
+                pltpu.VMEM((2 * nh - 1, 4, 1, WIDTH), F32),
                 pltpu.VMEM((2, 4, nh, WIDTH), F32),
                 pltpu.VMEM((4, nh, WIDTH), F32),
                 pltpu.VMEM((2 * nh, 8, WIDTH), F32),

time: 230 us -> 226 us (0.983)
  Pallas kernels: 229 us -> 225 us
    pallas_call x1, Pallas kernels: 226 us -> 222 us  [device_step(): pl.pallas_call(functools.partial(kernel, float(n_all)), out_shape=(pltpu....]
where the time goes in v6:
time: 226 us; the launch traced here: 225 us
  Pallas kernels  225 us (100%)
    pallas_call x1, Pallas kernels, device_step(): pl.pallas_call(functools.partial(kernel, float(n_all)), out_shape=(pltpu....  222 us

profile of v6, /device:TPU:0, one launch (start us, length us, event | category | flops | bytes accessed | tf_op | source)
XLA Modules:
  0.0 225.4 jit_solution(7539656111066731956)
XLA Ops:
  0.0 221.8 %mcl.1 = (f32[8,1024,256]{2,1,0:T(8,128)S(1)}, f32[1,2048]{1,0:T(1,128)S(1)}, bf16[7,4096,256]{2,1,0:T(8,128)(2,1)}) custom-call(f32[1024,2048]{1,0:T(8,128)} %flow_ref.1, f32[1024,2048]{1,0:T(8,128)} %graph_ref.1), custom_call_target="tpu_custom_call" | custom-call | tf_op jit(solution)/shard_map/mcl/pallas_call | solution.py:503
  221.8 3.4 %scale.1 = f32[1024,2048]{1,0:T(8,128)} custom-call(f32[8,1024,256]{2,1,0:T(8,128)S(1)} %get-tuple-element.7.raw_ref, f32[1,2048]{1,0:T(1,128)S(1)} %get-tuple-element.8.sum_ref), custom_call_target="tpu_custom_call" | custom-call | tf_op jit(solution)/shard_map/scale/pallas_call | solution.py:534

commit v7 on v6

--- a/solution.py
+++ b/solution.py
@@ -69,8 +69,8 @@
 
     def stage(j):
         if j < nh:
+            stage_copy(nh + j).start()
             stage_copy(j).start()
-            stage_copy(nh + j).start()
 
     gt[nh - 1] = jnp.zeros((kg_rows, WIDTH), BF16)
     stage(0)
@@ -80,26 +80,29 @@
     stage(1)
     stage(2)
 
-    def send_own(j):
+    def send_graph(j):
         block = gown.at[j, mine]
         remote(block, block, xown_s, xown_r.at[j], xn).start()
+        remote(block, block, cown_s, core_r.at[j], cn).start()
+
+    def send_flow(j):
         piece = pl.ds(j * WIDTH, WIDTH)
         remote(a0.at[:, piece], a0.at[:, pl.ds(cols + j * WIDTH, WIDTH)], ya_s, ya_r.at[j * 2 // nh], yn).start()
-        remote(block, block, cown_s, core_r.at[j], cn).start()
-
-    for j in range(nh):
-        with scope("cast"):
+
+    with scope("cast"):
+        for j in range(nh):
+            stage_copy(nh + j).wait()
+            a0[:, pl.ds(j * WIDTH, WIDTH)] = c1o[j].astype(BF16)
+            if j >= 1:
+                send_graph(j - 1)
             stage_copy(j).wait()
             gown[j, mine, :] = c1[j].astype(BF16)
-            stage_copy(nh + j).wait()
-            a0[:, pl.ds(j * WIDTH, WIDTH)] = c1o[j].astype(BF16)
+            if j == 0:
+                with scope("barrier"):
+                    pl.semaphore_wait(bar, 4)
+            send_flow(j)
             stage(j + 3)
-            if j == 1:
-                with scope('barrier'):
-                    pl.semaphore_wait(bar, 4)
-            if j >= 1:
-                send_own(j - 1)
-    send_own(nh - 1)
+    send_graph(nh - 1)
     for j in range(nf):
         for p in range(PIECES):
             src = gown.at[j, pl.ds(own + p * prow, prow)]
@@ -124,7 +127,7 @@
                 relay(jnp.int32(k), own, yg_s, yg_r, yn, True)
 
     def relayed(j):
-        return PIECES * j + 13 + lax.max(0, 6 - 4 * j)
+        return PIECES * j + 13 + lax.max(lax.max(0, 5 - 3 * j), 2 - 2 * lax.abs(j - 2))
 
     def relay_x(*ks):
         for k in ks:
@@ -194,19 +197,20 @@
         def _():
             wait_a(0)
 
-        @pl.when(j >= nh - 3)
-        def _():
             with scope("third_quarter"):
-                first = 2 * (j - (nh - 3))
-                third_quarter(first)
-                third_quarter(first + 1)
+                loop(0, nh - 3, third_quarter)
+
+        @pl.when(j > nh - 3)
+        def _():
+            with scope("third_quarter"):
+                third_quarter(j - 1)
     loop(0, nh, early)
     relay_y(0)
     with scope("early_end"):
-        third_quarter(nh - 2)
         first_half(nh - 1)
+    relay_y(1)
+    with scope("early_end"):
         third_quarter(nh - 1)
-    relay_y(1, 2)
     wait_a(1)
 
     def add_other(kg, j, g_tile):
@@ -231,7 +235,7 @@
             c1[q] = v
             sums[q, r] = jnp.sum(fold(v), axis=0, keepdims=True)
         send_sums(q)
-        for at, k in ((0, 3), (2, 4), (3, 5), (5, 6), (7, 7)):
+        for at, k in ((0, 2), (2, 3), (3, 4), (5, 5), (7, 6)):
             @pl.when(q == at)
             def _():
                 relay_y(k)
@@ -245,22 +249,22 @@
 
     def own_finish(q):
         finish(q, c1.at[q])
-        after(q, (1, 8), (3, 9), (7, 12))
+        after(q, (1, 7), (3, 8), (5, 11))
 
     def own_first(n):
         with scope("own_first"):
             c1[n] = dot(a1[:, :quad], gown[n, :quad, :])
-        after(n, (0, 10), (2, 11))
+        after(n, (0, 9), (2, 10))
 
     def own_second(n):
         with scope("own_second"):
             c1[n] += dot(a1[:, quad:cols], gown[n, quad:half, :])
-        after(n, (1, 13), (3, 14))
+        after(n, (0, 12), (2, 13))
 
     def own_whole(n):
         with scope("own_whole"):
             c1[n] = dot(a1[:, :cols], gown[n, :half, :])
-        relay_y(15 - nh // 2 + n)
+        relay_y(14 - nh // 2 + n)
     loop(0, nh // 2, own_finish)
     loop(0, nh // 2, own_first)
     loop(nh // 2, nh, own_finish)
@@ -271,13 +275,6 @@
     col_copy(nh).start()
     loop(nh // 2, nh, own_whole)
 
-    def right_own(kg):
-        def some(i):
-            for n in range(4):
-                c1[4 * i + n] += dot(a1[:, k_rows(kg)], gown[4 * i + n, k_rows(kg), :])
-        with scope("right_own"):
-            loop(0, nh // 4, some)
-
     def right_one(q):
         k_one = chunk(q)
 
@@ -301,8 +298,7 @@
         k = PIECES * j
         slot = lax.rem(q, 2)
         done = lax.div(q, 2)
-        at_last = j == nf - 2
-        paired = ((slot == 0) & (j > 0) & (j < nf - 1)) | at_last
+        paired = slot == 1
         kg = lax.div(q - 1, 2)
         pairs = lax.div(j + 1, 2)
         ahead = relayed(j)
@@ -336,7 +332,7 @@
         relay_ahead(1, 2)
         relay_next(0, 1, 2)
 
-        @pl.when((j > 0) & (j < nf - 1))
+        @pl.when(paired)
         def _():
             finish(q - 1, mbuf.at[1 - slot])
 
@@ -348,30 +344,34 @@
         relay_ahead(3)
         relay_next(3, 4)
 
-        @pl.when(at_last)
+        @pl.when(paired)
         def _():
             right_one(q - 1)
+            relay_ahead(4)
             finish(q, mbuf.at[slot])
             right_one(q)
-
-        @pl.when(paired & ~at_last)
-        def _():
-            right_own(kg)
-        relay_next(5)
-        relay_ahead(4)
-        relay_next(6)
-        relay_ahead(5)
-        relay_next(7)
+            relay_ahead(5)
+            relay_next(5, 6, 7)
+
+        @pl.when(~paired)
+        def _():
+            relay_next(5)
+            relay_ahead(4)
+            relay_next(6)
+            relay_ahead(5)
+            relay_next(7)
+
+        relay_ahead(6)
 
         @pl.when(j + 1 < nf)
         def _():
             wait_core(q + 1)
             col_copy(q + 1).start()
+        relay_ahead(7)
 
         @pl.when(paired)
         def _():
             right_other(kg, pairs)
-        relay_ahead(6, 7)
     loop(0, nf, other_step)
 
     last_kg = nh - 1

time: 226 us -> 224 us (level)
  no operation moved by 1% of the time
where the time goes in v7:
time: 224 us
  Pallas kernels  224 us (100%)
    pallas_call x1, Pallas kernels, device_step(): pl.pallas_call(functools.partial(kernel, float(n_all)), out_shape=(pltpu....  220 us

profile of v7, /device:TPU:0, one launch (start us, length us, event | category | flops | bytes accessed | tf_op | source)
XLA Modules:
  0.0 224.0 jit_solution(12113290328797871769)
XLA Ops:
  0.0 220.4 %mcl.1 = (f32[8,1024,256]{2,1,0:T(8,128)S(1)}, f32[1,2048]{1,0:T(1,128)S(1)}, bf16[7,4096,256]{2,1,0:T(8,128)(2,1)}) custom-call(f32[1024,2048]{1,0:T(8,128)} %flow_ref.1, f32[1024,2048]{1,0:T(8,128)} %graph_ref.1), custom_call_target="tpu_custom_call" | custom-call | tf_op jit(solution)/shard_map/mcl/pallas_call | solution.py:503
  220.4 3.4 %scale.1 = f32[1024,2048]{1,0:T(8,128)} custom-call(f32[8,1024,256]{2,1,0:T(8,128)S(1)} %get-tuple-element.7.raw_ref, f32[1,2048]{1,0:T(1,128)S(1)} %get-tuple-element.8.sum_ref), custom_call_target="tpu_custom_call" | custom-call | tf_op jit(solution)/shard_map/scale/pallas_call | solution.py:534

commit v8 on v7

--- a/solution.py
+++ b/solution.py
@@ -340,7 +340,13 @@
             c1o[j, m, :] = dot(a1[m, :cols], gcol[slot, :half, :])
         with scope("left"):
             over_m(expand_flow)
-            loop(nh // 2, done, lambda i: add_other(i, j, gcol.at[slot, k_rows(i)]))
+            twos = lax.div(done - nh // 2, 2)
+
+            def two(i):
+                k = pl.ds(pl.multiple_of(cols + i * 2 * kg_rows, 2 * kg_rows), 2 * kg_rows)
+                c1o[j] += dot(a1[:, k], gcol[slot, k, :])
+            loop(0, twos, two)
+            loop(nh // 2 + 2 * twos, done, lambda i: add_other(i, j, gcol.at[slot, k_rows(i)]))
         relay_ahead(3)
         relay_next(3, 4)
 

time: 224 us -> 224 us (level)
  no operation moved by 1% of the time
where the time goes in v8:
time: 224 us
  Pallas kernels  224 us (100%)
    pallas_call x1, Pallas kernels, device_step(): pl.pallas_call(functools.partial(kernel, float(n_all)), out_shape=(pltpu....  220 us

profile of v8, /device:TPU:0, one launch (start us, length us, event | category | flops | bytes accessed | tf_op | source)
XLA Modules:
  0.0 223.8 jit_solution(13585897316903719602)
XLA Ops:
  0.0 220.2 %mcl.1 = (f32[8,1024,256]{2,1,0:T(8,128)S(1)}, f32[1,2048]{1,0:T(1,128)S(1)}, bf16[7,4096,256]{2,1,0:T(8,128)(2,1)}) custom-call(f32[1024,2048]{1,0:T(8,128)} %flow_ref.1, f32[1024,2048]{1,0:T(8,128)} %graph_ref.1), custom_call_target="tpu_custom_call" | custom-call | tf_op jit(solution)/shard_map/mcl/pallas_call | solution.py:509
  220.2 3.4 %scale.1 = f32[1024,2048]{1,0:T(8,128)} custom-call(f32[8,1024,256]{2,1,0:T(8,128)S(1)} %get-tuple-element.7.raw_ref, f32[1,2048]{1,0:T(1,128)S(1)} %get-tuple-element.8.sum_ref), custom_call_target="tpu_custom_call" | custom-call | tf_op jit(solution)/shard_map/scale/pallas_call | solution.py:540
